TPU v7x, 32 devices: a 4x4x1 block of a 4x4x8 slice. The times are simulated.
32 devices in a mesh: fit: 1 (over z), comp: 4 (over y), pts: 8 (over x, core).
Axes of the slice: x: 4, y: 4, z: 1, core: 2. Of those that a mesh axis runs over, the one named last changes fastest.
The devices are a block of a 4x4x8 slice.
Arguments:
- points: bfloat16 [16384, 512], P(('fit', 'pts'))
- means_init: float32 [4096, 512], P(('fit', 'comp'))
- logw_init: float32 [4096], P(('fit', 'comp'))
- inv_temp: float32 [3], replicated
Outputs:
- output 1: float32 [4096, 512], P(('fit', 'comp'))
- output 2: float32 [4096], P(('fit', 'comp'))
- output 3: float32 [16384], P(('fit', 'pts'))
All inputs are finite; a program needn't handle non-finite values.
Results may differ from a plain program's by a relative error of at most 0.001.
Values are sent between devices in bfloat16 or wider.
A program may use at most 768 MiB of HBM per device.

v0:
```python
import jax
import jax.numpy as jnp
from jax import lax
from jax.sharding import PartitionSpec as P

PRIOR_ALPHA = 1e-3
COUNT_EPS = 1e-6


def solution(mesh):
    row_groups = mesh.shape["pts"]
    comp_groups = mesh.shape["comp"]

    def per_device(points, mean_vecs, log_w, inv_temp):
        n_total = points.shape[0] * row_groups
        k_total = mean_vecs.shape[0] * comp_groups
        x_sq = jnp.einsum("nd,nd->n", points, points, preferred_element_type=jnp.float32)
        log_norm = None
        for sweep_idx in range(inv_temp.shape[0]):
            mean_bf = mean_vecs.astype(jnp.bfloat16)
            mean_sq = jnp.sum(mean_vecs * mean_vecs, axis=1)
            cross_dot = jnp.einsum("nd,kd->nk", points, mean_bf, preferred_element_type=jnp.float32)
            logits = log_w[None, :] - inv_temp[sweep_idx] * (x_sq[:, None] - 2.0 * cross_dot + mean_sq[None, :])
            row_top = lax.pmax(jnp.max(logits, axis=1), "comp")
            exp_total = lax.psum(jnp.sum(jnp.exp(logits - row_top[:, None]), axis=1), "comp")
            log_norm = row_top + jnp.log(exp_total)
            resp_prob = jnp.exp(logits - log_norm[:, None])
            counts = jnp.sum(resp_prob, axis=0)
            stat_sums = jnp.einsum("nk,nd->kd", resp_prob.astype(jnp.bfloat16), points, preferred_element_type=jnp.float32)
            counts, stat_sums = lax.psum((counts, stat_sums), "pts")
            mean_vecs = stat_sums / (counts[:, None] + COUNT_EPS)
            log_w = jnp.log((counts + PRIOR_ALPHA) / (n_total + k_total * PRIOR_ALPHA))
        return mean_vecs, log_w, log_norm

    row_spec = P(("fit", "pts"))
    comp_spec = P(("fit", "comp"))
    return jax.shard_map(
        per_device,
        mesh=mesh,
        in_specs=(P(("fit", "pts"), None), P(("fit", "comp"), None), comp_spec, P()),
        out_specs=(P(("fit", "comp"), None), comp_spec, row_spec),
        check_vma=False,
    )
```

profile of v0, /device:TPU:97, one launch (start us, length us, event | category | flops | bytes accessed | tf_op | source)
XLA Modules:
  0.0 321.1 jit_solution(4919610461583159584)
XLA Ops:
  7.2 0.1 all-reduce.4.cloned.1.call-start
  7.2 1.4 fusion.19
  8.7 1.8 multiply_reduce_fusion.2
  10.5 2.1 fusion.12
  12.5 8.8 %fusion.20 = (f32[2048]{0:T(1024)S(1)}, f32[2048,1024]{0,1:T(8,128)}) fusion(f32[1024]{0:T(1024)S(1)} %multiply_reduce_fusion.2, bf16[2048,512]{1,0:T(8,128)(2,1)} %param.4, f32[1024,512]{1,0:T(8,128)} %param.5, f32[2048]{0:T(1024)S(1)} %fusion.12, f32[]{:T(128)} %bitcast, f32[1024]{0:T(1024)} %param.6), kind=kOutput, calls=%fused_computation.42 | convolution fusion | flops 2160588800 | bytes 12607492 | tf_op jit(solution)/shard_map/nd,kd->nk/dot_general | solution.py:22
  21.3 0.0 copy-start
  21.3 11.4 %pmax.21 = f32[2048]{0:T(1024)S(1)} all-reduce(f32[2048]{0:T(1024)S(1)} %get-tuple-element.12), channel_id=1, replica_groups=mesh['fit'=1,'comp'=4,'pts'=8] {'comp'}, use_global_device_ids=true, to_apply=%region_2.0 | all-reduce | flops 2048 | bytes 16384 | tf_op jit(solution)/shard_map/pmax | solution.py:24
  32.8 4.5 %exponential_reduce_fusion.2 = f32[2048]{0:T(1024)S(1)} fusion(f32[2048,1024]{0,1:T(8,128)} %get-tuple-element.13, f32[2048]{0:T(1024)S(1)} %pmax.21), kind=kLoop, calls=%fused_computation.7 | loop fusion | flops 4192256 | bytes 8404992 | tf_op jit(solution)/shard_map/reduce_sum | solution.py:25
  37.3 6.2 %psum.63 = f32[2048]{0:T(1024)S(1)} all-reduce(f32[2048]{0:T(1024)S(1)} %exponential_reduce_fusion.2), channel_id=1, replica_groups=mesh['fit'=1,'comp'=4,'pts'=8] {'comp'}, use_global_device_ids=true, to_apply=%region_4.0 | all-reduce | flops 2048 | bytes 16384 | tf_op jit(solution)/shard_map/psum | solution.py:25
  43.5 0.0 copy-done
  43.5 7.0 %fusion.10 = f32[1024,512]{1,0:T(8,128)} fusion(bf16[2048,512]{1,0:T(8,128)(2,1)S(1)} %copy-done, f32[2048,1024]{0,1:T(8,128)} %get-tuple-element.13, f32[2048]{0:T(1024)S(1)} %log_add_fusion.2), kind=kOutput, calls=%fused_computation.17 | convolution fusion | flops 2151677952 | bytes 12591104 | tf_op jit(solution)/shard_map/nk,nd->kd/dot_general | solution.py:29
  50.6 0.1 all-reduce.4.cloned.1.call-update
  50.6 0.1 all-reduce.6.cloned.1.call-start
  50.7 4.6 %fusion.1 = f32[1024]{0:T(1024)S(1)} fusion(f32[2048,1024]{0,1:T(8,128)} %get-tuple-element.13, f32[2048]{0:T(1024)S(1)} %log_add_fusion.2), kind=kLoop, calls=%fused_computation.10 | loop fusion | flops 4193280 | bytes 8400896 | tf_op jit(solution)/shard_map/reduce_sum | solution.py:28
  55.3 16.6 %psum.64 = f32[1024]{0:T(1024)S(1)} all-reduce(f32[1024]{0:T(1024)S(1)} %fusion.1), channel_id=1, replica_groups=mesh['fit'=1,'comp'=4,'pts'=8] {'pts'}, use_global_device_ids=true, to_apply=%region_6.0 | all-reduce | flops 1024 | bytes 8192 | tf_op jit(solution)/shard_map/psum | solution.py:30
  71.9 41.6 %all-reduce.4.cloned.1.call-done = f32[1024,512]{1,0:T(8,128)} async-done(((f32[1024,512]{1,0:T(8,128)}), f32[1024,512]{1,0:T(8,128)}) %all-reduce.4.cloned.1.call-update) | async-done | bytes 2097168 | tf_op jit(solution)/shard_map/psum | solution.py:30
  113.6 2.0 multiply_reduce_fusion.1
  115.5 8.1 %fusion.21 = (f32[2048]{0:T(1024)S(1)}, f32[1024,2048]{1,0:T(8,128)}) fusion(f32[1024]{0:T(1024)S(1)} %multiply_reduce_fusion.1, bf16[2048,512]{1,0:T(8,128)(2,1)S(1)} %copy-done, f32[1024,512]{1,0:T(8,128)} %all-reduce.4.cloned.1.call-done, f32[1024]{0:T(1024)S(1)} %get-tuple-element.7, f32[2048]{0:T(1024)S(1)} %fusion.12, f32[]{:T(128)} %bitcast.1, ...), kind=kOutput, calls=%fused_computation.43 | convolution fusion | flops 2161113088 | bytes 12611588 | tf_op jit(solution)/shard_map/nd,kd->nk/dot_general | solution.py:22
  123.6 9.1 %pmax.22 = f32[2048]{0:T(1024)S(1)} all-reduce(f32[2048]{0:T(1024)S(1)} %get-tuple-element.14), channel_id=1, replica_groups=mesh['fit'=1,'comp'=4,'pts'=8] {'comp'}, use_global_device_ids=true, to_apply=%region_10.0 | all-reduce | flops 2048 | bytes 16384 | tf_op jit(solution)/shard_map/pmax | solution.py:24
  132.8 4.5 %exponential_reduce_fusion.1 = f32[2048]{0:T(1024)S(1)} fusion(f32[1024,2048]{1,0:T(8,128)} %get-tuple-element.15, f32[2048]{0:T(1024)S(1)} %pmax.22), kind=kLoop, calls=%fused_computation.1 | loop fusion | flops 4192256 | bytes 8404992 | tf_op jit(solution)/shard_map/reduce_sum | solution.py:25
  137.3 6.2 %psum.66 = f32[2048]{0:T(1024)S(1)} all-reduce(f32[2048]{0:T(1024)S(1)} %exponential_reduce_fusion.1), channel_id=1, replica_groups=mesh['fit'=1,'comp'=4,'pts'=8] {'comp'}, use_global_device_ids=true, to_apply=%region_12.0 | all-reduce | flops 2048 | bytes 16384 | tf_op jit(solution)/shard_map/psum | solution.py:25
  143.5 7.1 %fusion.8 = f32[1024,512]{1,0:T(8,128)} fusion(bf16[2048,512]{1,0:T(8,128)(2,1)S(1)} %copy-done, f32[1024,2048]{1,0:T(8,128)} %get-tuple-element.15, f32[2048]{0:T(1024)S(1)} %log_add_fusion.1), kind=kOutput, calls=%fused_computation.16 | convolution fusion | flops 2151677952 | bytes 12591104 | tf_op jit(solution)/shard_map/nk,nd->kd/dot_general | solution.py:29
  150.6 0.1 all-reduce.6.cloned.1.call-update
  150.6 0.1 all-reduce.8.cloned.1.call-start
  150.7 4.6 %fusion.2 = f32[1024]{0:T(1024)S(1)} fusion(f32[1024,2048]{1,0:T(8,128)} %get-tuple-element.15, f32[2048]{0:T(1024)S(1)} %log_add_fusion.1), kind=kLoop, calls=%fused_computation.11 | loop fusion | flops 4193280 | bytes 8400896 | tf_op jit(solution)/shard_map/reduce_sum | solution.py:28
  155.3 18.0 %psum.67 = f32[1024]{0:T(1024)S(1)} all-reduce(f32[1024]{0:T(1024)S(1)} %fusion.2), channel_id=1, replica_groups=mesh['fit'=1,'comp'=4,'pts'=8] {'pts'}, use_global_device_ids=true, to_apply=%region_14.0 | all-reduce | flops 1024 | bytes 8192 | tf_op jit(solution)/shard_map/psum | solution.py:30
  173.3 39.2 %all-reduce.6.cloned.1.call-done = f32[1024,512]{1,0:T(8,128)} async-done(((f32[1024,512]{1,0:T(8,128)}), f32[1024,512]{1,0:T(8,128)}) %all-reduce.6.cloned.1.call-update) | async-done | bytes 2097168 | tf_op jit(solution)/shard_map/psum | solution.py:30
  212.5 2.0 multiply_reduce_fusion
  214.4 8.1 %fusion.22 = (f32[2048]{0:T(1024)S(1)}, f32[1024,2048]{1,0:T(8,128)}) fusion(f32[1024]{0:T(1024)S(1)} %multiply_reduce_fusion, bf16[2048,512]{1,0:T(8,128)(2,1)S(1)} %copy-done, f32[1024,512]{1,0:T(8,128)} %all-reduce.6.cloned.1.call-done, f32[1024]{0:T(1024)S(1)} %get-tuple-element.5, f32[2048]{0:T(1024)S(1)} %fusion.12, f32[]{:T(128)} %bitcast.2, ...), kind=kOutput, calls=%fused_computation.44 | convolution fusion | flops 2161113088 | bytes 12611588 | tf_op jit(solution)/shard_map/nd,kd->nk/dot_general | solution.py:22
  222.5 8.9 %pmax.23 = f32[2048]{0:T(1024)S(1)} all-reduce(f32[2048]{0:T(1024)S(1)} %get-tuple-element.16), channel_id=1, replica_groups=mesh['fit'=1,'comp'=4,'pts'=8] {'comp'}, use_global_device_ids=true, to_apply=%region_18.0 | all-reduce | flops 2048 | bytes 16384 | tf_op jit(solution)/shard_map/pmax | solution.py:24
  231.5 4.5 %exponential_reduce_fusion = f32[2048]{0:T(1024)S(1)} fusion(f32[1024,2048]{1,0:T(8,128)} %get-tuple-element.17, f32[2048]{0:T(1024)S(1)} %pmax.23), kind=kLoop, calls=%fused_computation | loop fusion | flops 4192256 | bytes 8404992 | tf_op jit(solution)/shard_map/reduce_sum | solution.py:25
  236.0 6.4 %psum.69 = f32[2048]{0:T(1024)S(1)} all-reduce(f32[2048]{0:T(1024)S(1)} %exponential_reduce_fusion), channel_id=1, replica_groups=mesh['fit'=1,'comp'=4,'pts'=8] {'comp'}, use_global_device_ids=true, to_apply=%region_20.0 | all-reduce | flops 2048 | bytes 16384 | tf_op jit(solution)/shard_map/psum | solution.py:25
  242.4 0.0 copy-start.1
  242.5 7.0 %fusion.6 = f32[1024,512]{1,0:T(8,128)} fusion(bf16[2048,512]{1,0:T(8,128)(2,1)S(1)} %copy-done, f32[1024,2048]{1,0:T(8,128)} %get-tuple-element.17, f32[2048]{0:T(1024)S(1)} %log_add_fusion), kind=kOutput, calls=%fused_computation.15 | convolution fusion | flops 2151677952 | bytes 12591104 | tf_op jit(solution)/shard_map/nk,nd->kd/dot_general | solution.py:29
  249.5 0.1 all-reduce.8.cloned.1.call-update
  249.6 0.0 copy-done.1
  249.6 4.6 %fusion.4 = f32[1024]{0:T(1024)S(1)} fusion(f32[1024,2048]{1,0:T(8,128)} %get-tuple-element.17, f32[2048]{0:T(1024)S(1)} %log_add_fusion), kind=kLoop, calls=%fused_computation.13 | loop fusion | flops 4193280 | bytes 8400896 | tf_op jit(solution)/shard_map/reduce_sum | solution.py:28
  254.1 18.0 %psum.71 = f32[1024]{0:T(1024)S(1)} all-reduce(f32[1024]{0:T(1024)S(1)} %fusion.4), channel_id=1, replica_groups=mesh['fit'=1,'comp'=4,'pts'=8] {'pts'}, use_global_device_ids=true, to_apply=%region_23.0 | all-reduce | flops 1024 | bytes 8192 | tf_op jit(solution)/shard_map/psum | solution.py:30
  272.2 0.6 multiply_log_fusion
  272.8 38.6 %all-reduce.8.cloned.1.call-done = f32[1024,512]{1,0:T(8,128)} async-done(((f32[1024,512]{1,0:T(8,128)}), f32[1024,512]{1,0:T(8,128)}) %all-reduce.8.cloned.1.call-update) | async-done | bytes 2097168 | tf_op jit(solution)/shard_map/psum | solution.py:30
  311.4 3.1 broadcast_divide_fusion
  (5 shorter events, 0.0 us)
Async XLA Ops:
  7.2 106.4 %all-reduce.4.cloned.1.call-start = ((), (), s32[]{:S(2)}) async-start(), calls=%async_computation | async-start | bytes 4194304 | tf_op jit(solution)/shard_map/psum | solution.py:30
  21.3 22.2 %copy-start = (bf16[2048,512]{1,0:T(8,128)(2,1)S(1)}, bf16[2048,512]{1,0:T(8,128)(2,1)}, u32[]{:S(2)}) copy-start(bf16[2048,512]{1,0:T(8,128)(2,1)} %param.4) | copy-start | bytes 6291460
  50.6 161.8 %all-reduce.6.cloned.1.call-start = ((), (), s32[]{:S(2)}) async-start(), calls=%async_computation.1 | async-start | bytes 4194304 | tf_op jit(solution)/shard_map/psum | solution.py:30
  150.6 160.8 %all-reduce.8.cloned.1.call-start = ((), (), s32[]{:S(2)}) async-start(), calls=%async_computation.2 | async-start | bytes 4194304 | tf_op jit(solution)/shard_map/psum | solution.py:30
  242.4 7.1 %copy-start.1 = (f32[2048]{0:T(1024)}, f32[2048]{0:T(1024)S(1)}, u32[]{:S(2)}) copy-start(f32[2048]{0:T(1024)S(1)} %log_add_fusion) | copy-start | bytes 24580
Sparse Core Ops, SparseCore 0:
  50.8 62.7 all-reduce.3
  150.8 61.6 all-reduce.5
  249.7 61.6 all-reduce.7
where the time goes:
time: 323 us; the launch traced here: 321 us
  waiting for transfers between devices  120 us (37%)
  blocking collectives  101 us (31%)
  matrix products  46.1 us (14%)
  other arithmetic  38.9 us (12%)
  between operations  13.9 us (4%)
    psum x3, waiting for transfers between devices, per_device(): counts, stat_sums = lax.psum((counts, stat_sums), 'pts')  119 us
    psum x3, blocking collectives, per_device(): counts, stat_sums = lax.psum((counts, stat_sums), 'pts')  52.7 us
    pmax x3, blocking collectives, per_device(): row_top = lax.pmax(jnp.max(logits, axis=1), 'comp')  29.5 us
    dot_general x3, matrix products, per_device(): jnp.einsum('nd,kd->nk', points, mean_bf, preferred_element_type=jnp.float32)  25 us
    dot_general x3, matrix products, per_device(): jnp.einsum('nk,nd->kd', resp_prob.astype(jnp.bfloat16), points, preferred...  21.1 us
    psum x3, blocking collectives, per_device(): lax.psum(jnp.sum(jnp.exp(logits - row_top[:, None]), axis=1), 'comp')  18.8 us
    reduce_sum x3, other arithmetic, per_device(): counts = jnp.sum(resp_prob, axis=0)  13.7 us
    reduce_sum x3, other arithmetic, per_device(): jnp.sum(jnp.exp(logits - row_top[:, None]), axis=1)  13.6 us
  transfers between devices with their start and end apart: 3, of which 3 were waited for; matrix products, arithmetic and copies ran while one was open for 4% of the time, Pallas kernels for 0%

commit v1 on v0

v1 whole, which is shorter than its diff:
```python
import functools
import math

import jax
import jax.numpy as jnp
from jax import lax
from jax.experimental import pallas as pl
from jax.experimental.pallas import tpu as pltpu
from jax.sharding import PartitionSpec as P

PRIOR_ALPHA = 1e-3
COUNT_EPS = 1e-6
LOG2E = math.log2(math.e)
LN2 = math.log(2.0)
MESH = pl.DeviceIdType.MESH
CORES = 2
LANES = 128

OPP, RIGHT, LEFT, OWN = range(4)
SHIFT = {OPP: 2, RIGHT: 1, LEFT: 3, OWN: 0}


def em_kernel(
    sweeps, n_total, k_total, n_chips, n_comp,
    beta_ref, x_hbm, mean_hbm, logw_ref,
    mean_out, logw_out, lse_out,
    x_all, xt, hq, e_buf, r_buf, mean_f, mean_b, prm, m_st, s_st, pair_out, pair_in, glob_out, glob_in,
    lse_own, lse_oth, s_buf, rs_in, acc_out, n_out, n_in, row_out, row_in, send_sem, recv_sem, copy_sem,
):
    n_loc, depth = x_all.shape[1], x_all.shape[2]
    kq = mean_f.shape[1]
    kh = kq // 2
    half = n_chips * kq

    p = lax.axis_index("pts")
    y = lax.axis_index("comp")
    chip = lax.div(p, CORES)
    core = p - chip * CORES
    partner = {"pts": chip * CORES + 1 - core}

    def x_peer(d):
        return {"pts": lax.rem(chip + d, n_chips) * CORES + core}

    right, left, opposite = x_peer(1), x_peer(n_chips - 1), x_peer(2)
    y_peers = [{"comp": lax.rem(y + d, n_comp)} for d in range(1, n_comp)]

    barrier = pltpu.get_barrier_semaphore()
    everyone = [partner, right, left, opposite] + y_peers
    for dev in everyone:
        pl.semaphore_signal(barrier, inc=1, device_id=dev, device_id_type=MESH)

    load_x = pltpu.make_async_copy(x_hbm, x_all.at[0], copy_sem.at[4])
    load_x.start()
    load_mean = []
    for b in range(4):
        q = lax.rem(chip + SHIFT[b], n_chips)
        c = pltpu.make_async_copy(
            mean_hbm.at[pl.ds(pl.multiple_of(core * half + q * kq, kq), kq)], mean_f.at[b], copy_sem.at[b]
        )
        c.start()
        load_mean.append(c)

    pending = []

    def send(src, dst, t, idx, dev):
        c = pltpu.make_async_remote_copy(
            src_ref=src, dst_ref=dst, send_sem=send_sem.at[t, idx], recv_sem=recv_sem.at[t, idx],
            device_id=dev, device_id_type=MESH,
        )
        c.start()
        pending.append(c)
        return c

    def drain():
        for c in pending:
            c.wait_send()
        pending.clear()

    eye = lax.broadcasted_iota(jnp.int32, (kq, kq), 0) == lax.broadcasted_iota(jnp.int32, (kq, kq), 1)

    def to_col(row):
        return jnp.sum(jnp.where(eye, jnp.broadcast_to(row, (kq, kq)), 0.0), axis=1, keepdims=True)

    def to_row(col):
        return jnp.sum(jnp.where(eye, jnp.broadcast_to(col, (kq, kq)), 0.0), axis=0, keepdims=True)

    pl.semaphore_wait(barrier, len(everyone))
    x_copy = send(x_hbm, x_all.at[1], 0, 31, partner)

    load_x.wait()
    for b in range(4):
        load_mean[b].wait()
        mf = mean_f[b]
        mean_b[0, b] = mf.astype(jnp.bfloat16)
        q = lax.rem(chip + SHIFT[b], n_chips)
        prm[0, b, 0:1, :] = logw_ref[pl.ds(core * n_chips + q, 1), :] * LOG2E
        prm[0, b, 1:2, :] = to_row(0.5 * jnp.sum(mf * mf, axis=1, keepdims=True))

    tr = min(512, n_loc)

    def prepare(h):
        @pl.loop(0, n_loc // tr)
        def _(c):
            rows = pl.ds(pl.multiple_of(c * tr, tr), tr)
            cols = pl.ds(pl.multiple_of(h * n_loc + c * tr, tr), tr)
            blk = x_all[h, rows, :].T
            xt[:, cols] = blk
            f = blk.astype(jnp.float32)
            hq[:, cols] = 0.5 * jnp.sum(f * f, axis=0, keepdims=True)

    tile = min(256, n_loc)
    unroll = min(4, n_loc // tile)

    def a_phase(t, h, blocks):
        neg_beta2 = beta_ref[t] * (-2.0 * LOG2E)
        lp = [to_col(prm[t, b, 0:1, :]) for b in blocks]
        hm = [to_col(prm[t, b, 1:2, :]) for b in blocks]
        lo, nb = blocks[0], len(blocks)

        @pl.loop(0, n_loc // (tile * unroll))
        def _(c):
            for u in range(unroll):
                cols = pl.ds(pl.multiple_of(h * n_loc + (c * unroll + u) * tile, tile), tile)
                means = mean_b[t, lo:lo + nb].reshape(nb * kq, depth)
                a_all = jnp.dot(means, xt[:, cols], preferred_element_type=jnp.float32)
                hqc = hq[:, cols]
                for i, b in enumerate(blocks):
                    a = a_all[i * kq:(i + 1) * kq]
                    logit = ((hqc - a) + hm[i]) * neg_beta2 + lp[i]
                    m = jnp.max(logit, axis=0, keepdims=True)
                    e = jnp.exp2(logit - m)
                    e_buf[b * kq:(b + 1) * kq, cols] = e
                    m_st[b:b + 1, cols] = m
                    s_st[b:b + 1, cols] = jnp.sum(e, axis=0, keepdims=True)

    def local_pair(h):
        cols = pl.ds(h * n_loc, n_loc)
        ms = [m_st[b:b + 1, cols] for b in range(4)]
        m = jnp.maximum(jnp.maximum(ms[0], ms[1]), jnp.maximum(ms[2], ms[3]))
        s = sum(s_st[b:b + 1, cols] * jnp.exp2(ms[b] - m) for b in range(4))
        return m, s

    def r_phase(h, blocks, lse, accs):
        rt = min(512, n_loc)

        def body(c, acc):
            acc = list(acc)
            cols = pl.ds(pl.multiple_of(h * n_loc + c * rt, rt), rt)
            l2 = lse[:, pl.ds(pl.multiple_of(c * rt, rt), rt)]
            for i, b in enumerate(blocks):
                f = jnp.exp2(m_st[b:b + 1, cols] - l2)
                r = e_buf[b * kq:(b + 1) * kq, cols] * f
                r_buf[b * kq:(b + 1) * kq, cols] = r.astype(jnp.bfloat16)
                for v in range(rt // LANES):
                    acc[i] = acc[i] + r[:, v * LANES:(v + 1) * LANES]
            return tuple(acc)

        return lax.fori_loop(0, n_loc // rt, body, accs)

    zero = jnp.zeros((kq, LANES), jnp.float32)

    for t in range(sweeps):
        last = t == sweeps - 1
        if t == 0:
            prepare(0)
            for pair in ((0, 1), (2, 3)):
                a_phase(t, 0, pair)
            x_copy.wait_recv()
            prepare(1)
            for pair in ((0, 1), (2, 3)):
                a_phase(t, 1, pair)
        else:
            gather[1].wait_recv()
            gather[6].wait_recv()
            a_phase(t, 1, (LEFT,))
            a_phase(t, 0, (LEFT,))
            gather[4].wait_recv()
            gather[7].wait_recv()
            a_phase(t, 1, (RIGHT,))
            a_phase(t, 0, (RIGHT,))
            gather[2].wait_recv()
            gather[5].wait_recv()
            gather[8].wait_recv()
            a_phase(t, 1, (OPP,))
        m, s = local_pair(1)
        pair_out[t, 0:1, :] = m
        pair_out[t, 1:2, :] = s
        pair = send(pair_out.at[t], pair_in.at[t], t, 0, partner)
        if t > 0:
            a_phase(t, 0, (OPP,))
        m, s = local_pair(0)
        pair.wait_recv()
        m1, s1 = pair_in[t, 0:1, :], pair_in[t, 1:2, :]
        top = jnp.maximum(m, m1)
        s = s * jnp.exp2(m - top) + s1 * jnp.exp2(m1 - top)
        glob_out[t, 0:1, :] = top
        glob_out[t, 1:2, :] = s
        across = [
            send(glob_out.at[t], glob_in.at[t, d], t, 1 + d, y_peers[d]) for d in range(n_comp - 1)
        ]
        tops, sums = [top], [s]
        for d in range(n_comp - 1):
            across[d].wait_recv()
            tops.append(glob_in[t, d, 0:1, :])
            sums.append(glob_in[t, d, 1:2, :])
        top = functools.reduce(jnp.maximum, tops)
        total = sum(v * jnp.exp2(w - top) for v, w in zip(sums, tops))
        lse2 = top + jnp.log(total) * LOG2E
        lse_own[t] = lse2
        swap = send(lse_own.at[t], lse_oth.at[t], t, 4, partner)
        if last:
            lse_out[...] = lse2 * LN2

        own_r = lse_own.at[t]
        accs = r_phase(0, (0, 1, 2, 3), own_r, (zero,) * 4)
        swap.wait_recv()
        oth_r = lse_oth.at[t]
        acc_a = r_phase(1, (0, 1), oth_r, accs[:2])
        counts = []

        def stats(lo):
            out = jnp.dot(
                r_buf[lo * kq:(lo + 2) * kq, 0:n_loc], x_all[0], preferred_element_type=jnp.float32
            )
            out += jnp.dot(
                r_buf[lo * kq:(lo + 2) * kq, n_loc:2 * n_loc], x_all[1], preferred_element_type=jnp.float32
            )
            s_buf[t, 2 * lo:2 * lo + 4] = out.reshape(4, kh, depth)

        stats(0)
        scat = [
            send(s_buf.at[t, 2 * OPP], rs_in.at[t, 0], t, 5, right),
            send(s_buf.at[t, 2 * OPP + 1], rs_in.at[t, 1], t, 6, left),
            send(s_buf.at[t, 2 * RIGHT + 1], rs_in.at[t, 2], t, 7, right),
        ]
        acc_b = r_phase(1, (2, 3), oth_r, accs[2:])
        for b, acc in enumerate(tuple(acc_a) + tuple(acc_b)):
            row = to_row(jnp.sum(acc, axis=1, keepdims=True))
            n_out[t, b, 0:1, :] = row
            counts.append(row)
        n_copies = [
            send(n_out.at[t, OPP], n_in.at[t, 0], t, 8, opposite),
            send(n_out.at[t, RIGHT], n_in.at[t, 1], t, 9, right),
            send(n_out.at[t, LEFT], n_in.at[t, 2], t, 10, left),
        ]
        stats(2)
        scat.append(send(s_buf.at[t, 2 * LEFT], rs_in.at[t, 3], t, 11, left))
        scat[0].wait_recv()
        acc_out[t, 0] = s_buf[t, 2 * RIGHT] + rs_in[t, 0]
        scat.append(send(acc_out.at[t, 0], rs_in.at[t, 4], t, 12, right))
        scat[1].wait_recv()
        acc_out[t, 1] = s_buf[t, 2 * LEFT + 1] + rs_in[t, 1]
        scat.append(send(acc_out.at[t, 1], rs_in.at[t, 5], t, 13, left))

        n_row = counts[OWN]
        for d in range(3):
            n_copies[d].wait_recv()
            n_row = n_row + n_in[t, d, 0:1, :]
        n_col = to_col(n_row) + COUNT_EPS
        logw = jnp.log((n_row + PRIOR_ALPHA) / (n_total + k_total * PRIOR_ALPHA))

        scat[3].wait_recv()
        scat[4].wait_recv()
        mean_lo = (s_buf[t, 2 * OWN] + rs_in[t, 3] + rs_in[t, 4]) / n_col[:kh]
        if not last:
            nxt = mean_b.at[t + 1]
            a_rows, b_rows = pl.ds(0, kh), pl.ds(kh, kh)
            mean_b[t + 1, OWN, 0:kh, :] = mean_lo.astype(jnp.bfloat16)
            mine_a, mine_b = nxt.at[OWN, a_rows], nxt.at[OWN, b_rows]
            g0 = send(mine_a, nxt.at[LEFT, a_rows], t, 14, right)
            scat[2].wait_recv()
            scat[5].wait_recv()
            mean_hi = (s_buf[t, 2 * OWN + 1] + rs_in[t, 2] + rs_in[t, 5]) / n_col[kh:]
            mean_b[t + 1, OWN, kh:kq, :] = mean_hi.astype(jnp.bfloat16)
            g3 = send(mine_b, nxt.at[RIGHT, b_rows], t, 17, left)
            g1 = send(mine_b, nxt.at[LEFT, b_rows], t, 15, right)
            g4 = send(mine_a, nxt.at[RIGHT, a_rows], t, 18, left)
            sq = jnp.concatenate(
                [jnp.sum(mean_lo * mean_lo, axis=1, keepdims=True), jnp.sum(mean_hi * mean_hi, axis=1, keepdims=True)], axis=0
            )
            prm[t + 1, OWN, 0:1, :] = logw * LOG2E
            prm[t + 1, OWN, 1:2, :] = to_row(0.5 * sq)
            src = prm.at[t + 1, OWN]
            g6 = send(src, prm.at[t + 1, LEFT], t, 20, right)
            g7 = send(src, prm.at[t + 1, RIGHT], t, 21, left)
            g8 = send(src, prm.at[t + 1, OPP], t, 22, opposite)
            a_phase(t + 1, 1, (OWN,))
            a_phase(t + 1, 0, (OWN,))
            g0.wait_recv()
            g2 = send(nxt.at[LEFT, a_rows], nxt.at[OPP, a_rows], t, 16, right)
            g3.wait_recv()
            g5 = send(nxt.at[RIGHT, b_rows], nxt.at[OPP, b_rows], t, 19, left)
            gather = [g0, g1, g2, g3, g4, g5, g6, g7, g8]
        else:
            def rows(shift, upper):
                q = lax.rem(chip + shift, n_chips)
                at = pl.multiple_of(core * half + q * kq + (kh if upper else 0), kh)
                return mean_out.at[pl.ds(at, kh)]

            def forward(shift, upper, idx, dev):
                return send(rows(shift, upper), rows(shift, upper), t, idx, dev)

            rows(0, False)[...] = mean_lo
            f0 = forward(0, False, 14, right)
            scat[2].wait_recv()
            scat[5].wait_recv()
            rows(0, True)[...] = (s_buf[t, 2 * OWN + 1] + rs_in[t, 2] + rs_in[t, 5]) / n_col[kh:]
            f3 = forward(0, True, 17, left)
            f1 = forward(0, True, 15, right)
            f4 = forward(0, False, 18, left)
            row_out[OWN, 0:1, :] = logw
            src = row_out.at[OWN]
            r6 = send(src, row_out.at[LEFT], t, 20, right)
            r7 = send(src, row_out.at[RIGHT], t, 21, left)
            r8 = send(src, row_out.at[OPP], t, 22, opposite)
            d2d = [forward(0, False, 23, partner), forward(0, True, 24, partner)]
            f0.wait_recv()
            f2 = forward(3, False, 16, right)
            d2d.append(forward(3, False, 25, partner))
            f3.wait_recv()
            f5 = forward(1, True, 19, left)
            d2d.append(forward(1, True, 26, partner))
            for c in (r6, r7, r8):
                c.wait_recv()
            rows_copy = send(row_out, row_in, t, 30, partner)
            f1.wait_recv()
            d2d.append(forward(3, True, 27, partner))
            f4.wait_recv()
            d2d.append(forward(1, False, 28, partner))
            f2.wait_recv()
            d2d.append(forward(2, False, 29, partner))
            f5.wait_recv()
            d2d.append(forward(2, True, 32, partner))
            rows_copy.wait_recv()
            for b in range(4):
                q = lax.rem(chip + SHIFT[b], n_chips)
                logw_out[pl.ds(core * n_chips + q, 1), :] = row_out[b, 0:1, :]
                logw_out[pl.ds((1 - core) * n_chips + q, 1), :] = row_in[b, 0:1, :]
            for c in d2d:
                c.wait_recv()
        drain()


def solution(mesh):
    n_pts, n_comp = mesh.shape["pts"], mesh.shape["comp"]
    n_chips = n_pts // CORES

    def per_device(points, means, log_w, inv_temp):
        n_loc, depth = points.shape
        k_loc = means.shape[0]
        kq = k_loc // n_pts
        half = n_chips * kq
        sweeps = inv_temp.shape[0]
        if n_chips != 4 or kq != LANES:
            raise ValueError("unsupported shape")
        f32, bf16 = jnp.float32, jnp.bfloat16
        kernel = functools.partial(
            em_kernel, sweeps, n_loc * n_pts, k_loc * n_comp, n_chips, n_comp
        )
        vmem = pl.BlockSpec(memory_space=pltpu.VMEM)
        anywhere = pl.BlockSpec(memory_space=pl.ANY)
        V = pltpu.VMEM
        mean, logw, lse = pl.pallas_call(
            kernel,
            out_shape=(
                jax.ShapeDtypeStruct((k_loc, depth), f32),
                jax.ShapeDtypeStruct((n_pts, kq), f32),
                jax.ShapeDtypeStruct((1, n_loc), f32),
            ),
            in_specs=[pl.BlockSpec(memory_space=pltpu.SMEM), anywhere, anywhere, vmem],
            out_specs=(vmem, vmem, vmem),
            scratch_shapes=[
                V((2, n_loc, depth), bf16),
                V((depth, 2 * n_loc), bf16),
                V((1, 2 * n_loc), f32),
                V((half, 2 * n_loc), f32),
                V((half, 2 * n_loc), bf16),
                V((4, kq, depth), f32),
                V((sweeps, 4, kq, depth), bf16),
                V((sweeps, 4, 8, kq), f32),
                V((4, 2 * n_loc), f32),
                V((4, 2 * n_loc), f32),
                V((sweeps, 2, n_loc), f32),
                V((sweeps, 2, n_loc), f32),
                V((sweeps, 2, n_loc), f32),
                V((sweeps, n_comp - 1, 2, n_loc), f32),
                V((sweeps, 1, n_loc), f32),
                V((sweeps, 1, n_loc), f32),
                V((sweeps, 8, kq // 2, depth), f32),
                V((sweeps, 6, kq // 2, depth), f32),
                V((sweeps, 2, kq // 2, depth), f32),
                V((sweeps, 4, 8, kq), f32),
                V((sweeps, 3, 8, kq), f32),
                V((4, 8, kq), f32),
                V((4, 8, kq), f32),
                pltpu.SemaphoreType.DMA((sweeps, 33)),
                pltpu.SemaphoreType.DMA((sweeps, 33)),
                pltpu.SemaphoreType.DMA((5,)),
            ],
            compiler_params=pltpu.CompilerParams(
                collective_id=0, has_side_effects=True, vmem_limit_bytes=60 * 1024 * 1024
            ),
            name="em",
        )(inv_temp, points, means, log_w.reshape(n_pts, kq))
        return mean, logw.reshape(k_loc), lse.reshape(n_loc)

    comp_spec = P(("fit", "comp"))
    return jax.shard_map(
        per_device,
        mesh=mesh,
        in_specs=(P(("fit", "pts"), None), P(("fit", "comp"), None), comp_spec, P()),
        out_specs=(P(("fit", "comp"), None), comp_spec, P(("fit", "pts"))),
        check_vma=False,
    )
```

time: 323 us -> 113 us (0.35)
  waiting for transfers between devices: 120 us -> 0 us
  Pallas kernels: 0 us -> 107 us
  blocking collectives: 101 us -> 0 us
  matrix products: 46.1 us -> 0 us
  other arithmetic: 38.9 us -> 0 us
  between operations: 13.9 us -> 0.66 us
    psum x3 -> x0, waiting for transfers between devices: 119 us -> none  [per_device(): counts, stat_sums = lax.psum((counts, stat_sums), 'pts')]
    pallas_call x0 -> x1, Pallas kernels: none -> 107 us  [per_device(): pl.pallas_call(kernel, out_shape=(jax.ShapeDtypeStruct((k_loc, depth), f3...]
    psum x6 -> x0, blocking collectives: 71.4 us -> none  [the longest x3 52.7 us: per_device(): counts, stat_sums = lax.psum((counts, stat_sums), 'pts')]
    dot_general x6 -> x0, matrix products: 46.1 us -> none  [the longest x3 25 us: per_device(): jnp.einsum('nd,kd->nk', points, mean_bf, preferred_element_type=jnp.float32)]
    reduce_sum x9 -> x0, other arithmetic: 33.1 us -> none  [the longest x3 13.7 us: per_device(): counts = jnp.sum(resp_prob, axis=0)]
    pmax x3 -> x0, blocking collectives: 29.5 us -> none  [per_device(): row_top = lax.pmax(jnp.max(logits, axis=1), 'comp')]
    unnamed x4 -> x7, local copies, waits for them, and re-layouts: 0.01 us -> 4.29 us
  transfers between devices with their start and end apart: 3 -> 0, of which waited for: 3 -> 0; matrix products, arithmetic and copies ran while one was open for 4% -> 0% of each run, Pallas kernels for 0% -> 0%
where the time goes in v1:
time: 113 us; the launch traced here: 112 us
  Pallas kernels  107 us (95%)
  local copies, waits for them, and re-layouts  4.29 us (4%)
    pallas_call x1, Pallas kernels, per_device(): pl.pallas_call(kernel, out_shape=(jax.ShapeDtypeStruct((k_loc, depth), f3...  107 us
    unnamed x7, local copies, waits for them, and re-layouts  4.29 us

profile of v1, /device:TPU:97, one launch (start us, length us, event | category | flops | bytes accessed | tf_op | source)
XLA Modules:
  0.0 112.4 jit_solution(2165483392834212378)
XLA Ops:
  0.6 107.5 %em.1 = (f32[1024,512]{1,0:T(8,128)}, f32[8,128]{1,0:T(8,128)}, f32[1,2048]{1,0:T(1,128)}) custom-call(f32[3]{0:T(128)} %beta_ref.1, bf16[2048,512]{1,0:T(8,128)(2,1)} %x_hbm.1, f32[1024,512]{1,0:T(8,128)} %mean_hbm.1, f32[8,128]{1,0:T(8,128)} %bitcast.4), custom_call_target="tpu_custom_call" | custom-call | tf_op jit(solution)/shard_map/em/pallas_call | solution.py:363
  108.1 0.0 copy-start.1
  108.1 0.0 copy-start
  108.2 3.1 %copy.10 = f32[1024,512]{1,0:T(8,128)} copy(f32[1024,512]{1,0:T(8,128)} %get-tuple-element.12) | data formatting | bytes 4194304
  111.2 0.0 copy-done.1
  111.2 0.6 copy.11
  111.8 0.0 copy-done
  111.8 0.6 copy.12
Async XLA Ops:
  108.1 3.1 %copy-start.1 = (f32[8,128]{1,0:T(8,128)S(1)}, f32[8,128]{1,0:T(8,128)}, u32[]{:S(2)}) copy-start(f32[8,128]{1,0:T(8,128)} %get-tuple-element.7) | copy-start | bytes 12292
  108.1 3.7 %copy-start = (f32[1,2048]{1,0:T(1,128)S(1)}, f32[1,2048]{1,0:T(1,128)}, u32[]{:S(2)}) copy-start(f32[1,2048]{1,0:T(1,128)} %get-tuple-element.8) | copy-start | bytes 24580

commit v2 on v1

--- a/solution.py
+++ b/solution.py
@@ -1,3 +1,4 @@
+import contextlib
 import functools
 import math
 
@@ -13,6 +14,7 @@
 LOG2E = math.log2(math.e)
 LN2 = math.log(2.0)
 MESH = pl.DeviceIdType.MESH
+scope = contextlib.nullcontext
 CORES = 2
 LANES = 128
 
@@ -22,11 +24,12 @@
 
 def em_kernel(
     sweeps, n_total, k_total, n_chips, n_comp,
-    beta_ref, x_hbm, mean_hbm, logw_ref,
+    beta_hbm, x_hbm, mean_hbm, logw_hbm,
     mean_out, logw_out, lse_out,
-    x_all, xt, hq, e_buf, r_buf, mean_f, mean_b, prm, m_st, s_st, pair_out, pair_in, glob_out, glob_in,
-    lse_own, lse_oth, s_buf, rs_in, acc_out, n_out, n_in, row_out, row_in, send_sem, recv_sem, copy_sem,
+    beta_ref, logw_ref, x_all, xt, hq, e_buf, r_buf, mean_f, mean_b, prm, m_st, s_st, pair_out, pair_in, glob_out, glob_in,
+    lse_own, lse_oth, cols_lp, cols_hm, raw_0, raw_1, s_buf, rs_in, acc_out, n_out, n_in, row_out, row_in, send_sem, recv_sem, copy_sem,
 ):
+    raw = (raw_0, raw_1)
     n_loc, depth = x_all.shape[1], x_all.shape[2]
     kq = mean_f.shape[1]
     kh = kq // 2
@@ -49,8 +52,11 @@
     for dev in everyone:
         pl.semaphore_signal(barrier, inc=1, device_id=dev, device_id_type=MESH)
 
-    load_x = pltpu.make_async_copy(x_hbm, x_all.at[0], copy_sem.at[4])
-    load_x.start()
+    load_small = [
+        pltpu.make_async_copy(logw_hbm, logw_ref, copy_sem.at[5]), pltpu.make_async_copy(beta_hbm, beta_ref, copy_sem.at[6])
+    ]
+    for c in load_small:
+        c.start()
     load_mean = []
     for b in range(4):
         q = lax.rem(chip + SHIFT[b], n_chips)
@@ -60,6 +66,9 @@
         c.start()
         load_mean.append(c)
 
+    load_x = pltpu.make_async_copy(x_hbm, x_all.at[0], copy_sem.at[4])
+    load_x.start()
+
     pending = []
 
     def send(src, dst, t, idx, dev):
@@ -84,54 +93,65 @@
     def to_row(col):
         return jnp.sum(jnp.where(eye, jnp.broadcast_to(col, (kq, kq)), 0.0), axis=0, keepdims=True)
 
-    pl.semaphore_wait(barrier, len(everyone))
-    x_copy = send(x_hbm, x_all.at[1], 0, 31, partner)
-
-    load_x.wait()
-    for b in range(4):
-        load_mean[b].wait()
-        mf = mean_f[b]
-        mean_b[0, b] = mf.astype(jnp.bfloat16)
-        q = lax.rem(chip + SHIFT[b], n_chips)
-        prm[0, b, 0:1, :] = logw_ref[pl.ds(core * n_chips + q, 1), :] * LOG2E
-        prm[0, b, 1:2, :] = to_row(0.5 * jnp.sum(mf * mf, axis=1, keepdims=True))
+    with scope("loads"):
+        for c in load_small:
+            c.wait()
+    with scope("meanprep"):
+        for b in range(4):
+            load_mean[b].wait()
+            mf = mean_f[b]
+            mean_b[0, b] = mf.astype(jnp.bfloat16)
+            q = lax.rem(chip + SHIFT[b], n_chips)
+            prm[0, b, 0:1, :] = logw_ref[pl.ds(core * n_chips + q, 1), :] * LOG2E
+            prm[0, b, 1:2, :] = to_row(0.5 * jnp.sum(mf * mf, axis=1, keepdims=True))
 
     tr = min(512, n_loc)
-
-    def prepare(h):
-        @pl.loop(0, n_loc // tr)
-        def _(c):
-            rows = pl.ds(pl.multiple_of(c * tr, tr), tr)
-            cols = pl.ds(pl.multiple_of(h * n_loc + c * tr, tr), tr)
-            blk = x_all[h, rows, :].T
-            xt[:, cols] = blk
-            f = blk.astype(jnp.float32)
-            hq[:, cols] = 0.5 * jnp.sum(f * f, axis=0, keepdims=True)
+    n_tr = n_loc // tr
+
+    def prepare(h, c):
+        cols = slice(h * n_loc + c * tr, h * n_loc + (c + 1) * tr)
+        blk = x_all[h, c * tr:(c + 1) * tr, :].T
+        xt[:, cols] = blk
+        f = blk.astype(jnp.float32)
+        hq[:, cols] = 0.5 * jnp.sum(f * f, axis=0, keepdims=True)
 
     tile = min(256, n_loc)
-    unroll = min(4, n_loc // tile)
-
-    def a_phase(t, h, blocks):
+
+    def columns(t, blocks):
+        for b in blocks:
+            cols_lp[b] = jnp.broadcast_to(to_col(prm[t, b, 0:1, :]), (kq, LANES))
+            cols_hm[b] = jnp.broadcast_to(to_col(prm[t, b, 1:2, :]), (kq, LANES))
+
+    def a_phase(t, tiles, blocks):
         neg_beta2 = beta_ref[t] * (-2.0 * LOG2E)
-        lp = [to_col(prm[t, b, 0:1, :]) for b in blocks]
-        hm = [to_col(prm[t, b, 1:2, :]) for b in blocks]
         lo, nb = blocks[0], len(blocks)
-
-        @pl.loop(0, n_loc // (tile * unroll))
-        def _(c):
-            for u in range(unroll):
-                cols = pl.ds(pl.multiple_of(h * n_loc + (c * unroll + u) * tile, tile), tile)
-                means = mean_b[t, lo:lo + nb].reshape(nb * kq, depth)
-                a_all = jnp.dot(means, xt[:, cols], preferred_element_type=jnp.float32)
+        means = mean_b.at[t, lo:lo + nb]
+
+        def product(u):
+            cols = slice(tiles[u] * tile, (tiles[u] + 1) * tile)
+            raw[u % 2][0:nb * kq] = jnp.dot(
+                means[...].reshape(nb * kq, depth), xt[:, cols], preferred_element_type=jnp.float32
+            )
+
+        product(0)
+        for u in range(len(tiles)):
+            if u + 1 < len(tiles):
+                product(u + 1)
+            for v in range(tile // LANES):
+                at = tiles[u] * tile + v * LANES
+                cols = slice(at, at + LANES)
                 hqc = hq[:, cols]
                 for i, b in enumerate(blocks):
-                    a = a_all[i * kq:(i + 1) * kq]
-                    logit = ((hqc - a) + hm[i]) * neg_beta2 + lp[i]
+                    a = raw[u % 2][i * kq:(i + 1) * kq, v * LANES:(v + 1) * LANES]
+                    logit = ((hqc - a) + cols_hm[b]) * neg_beta2 + cols_lp[b]
                     m = jnp.max(logit, axis=0, keepdims=True)
                     e = jnp.exp2(logit - m)
                     e_buf[b * kq:(b + 1) * kq, cols] = e
                     m_st[b:b + 1, cols] = m
                     s_st[b:b + 1, cols] = jnp.sum(e, axis=0, keepdims=True)
+
+    per_half = n_loc // tile
+    tiles_of = [list(range(per_half)), list(range(per_half, 2 * per_half))]
 
     def local_pair(h):
         cols = pl.ds(h * n_loc, n_loc)
@@ -162,34 +182,53 @@
     for t in range(sweeps):
         last = t == sweeps - 1
         if t == 0:
-            prepare(0)
-            for pair in ((0, 1), (2, 3)):
-                a_phase(t, 0, pair)
-            x_copy.wait_recv()
-            prepare(1)
-            for pair in ((0, 1), (2, 3)):
-                a_phase(t, 1, pair)
+            columns(0, range(4))
+            with scope("loadx"):
+                load_x.wait()
+            with scope("prep0"):
+                for c in range(n_tr):
+                    prepare(0, c)
+            with scope("barrier"):
+                pl.semaphore_wait(barrier, len(everyone))
+            x_rows = [pl.ds(c * tr, tr) for c in range(n_tr)]
+            x_copies = [send(x_hbm.at[r], x_all.at[1, r], 0, 33 + c, partner) for c, r in enumerate(x_rows)]
+            with scope("a00"):
+                a_phase(t, tiles_of[0], range(4))
+            per_tr = tr // tile
+            for c in range(n_tr):
+                with scope("xwait"):
+                    x_copies[c].wait_recv()
+                with scope("prep1"):
+                    prepare(1, c)
+                with scope("a01"):
+                    a_phase(t, tiles_of[1][c * per_tr:(c + 1) * per_tr], range(4))
         else:
-            gather[1].wait_recv()
-            gather[6].wait_recv()
-            a_phase(t, 1, (LEFT,))
-            a_phase(t, 0, (LEFT,))
-            gather[4].wait_recv()
-            gather[7].wait_recv()
-            a_phase(t, 1, (RIGHT,))
-            a_phase(t, 0, (RIGHT,))
-            gather[2].wait_recv()
-            gather[5].wait_recv()
-            gather[8].wait_recv()
-            a_phase(t, 1, (OPP,))
+            with scope("wait_left"):
+                gather[1].wait_recv()
+                gather[6].wait_recv()
+            with scope("wait_right"):
+                gather[4].wait_recv()
+                gather[7].wait_recv()
+            with scope("a_right"):
+                columns(t, (RIGHT, LEFT))
+                a_phase(t, tiles_of[1] + tiles_of[0], (RIGHT, LEFT))
+            with scope("wait_opp"):
+                gather[2].wait_recv()
+                gather[5].wait_recv()
+                gather[8].wait_recv()
+            with scope("a_opp1"):
+                columns(t, (OPP,))
+                a_phase(t, tiles_of[1], (OPP,))
         m, s = local_pair(1)
         pair_out[t, 0:1, :] = m
         pair_out[t, 1:2, :] = s
         pair = send(pair_out.at[t], pair_in.at[t], t, 0, partner)
         if t > 0:
-            a_phase(t, 0, (OPP,))
+            with scope("a_opp0"):
+                a_phase(t, tiles_of[0], (OPP,))
         m, s = local_pair(0)
-        pair.wait_recv()
+        with scope("wait_pair"):
+            pair.wait_recv()
         m1, s1 = pair_in[t, 0:1, :], pair_in[t, 1:2, :]
         top = jnp.maximum(m, m1)
         s = s * jnp.exp2(m - top) + s1 * jnp.exp2(m1 - top)
@@ -200,7 +239,8 @@
         ]
         tops, sums = [top], [s]
         for d in range(n_comp - 1):
-            across[d].wait_recv()
+            with scope("wait_y"):
+                across[d].wait_recv()
             tops.append(glob_in[t, d, 0:1, :])
             sums.append(glob_in[t, d, 1:2, :])
         top = functools.reduce(jnp.maximum, tops)
@@ -209,13 +249,18 @@
         lse_own[t] = lse2
         swap = send(lse_own.at[t], lse_oth.at[t], t, 4, partner)
         if last:
-            lse_out[...] = lse2 * LN2
+            lse = lse2 * LN2
+            for i in range(n_loc // LANES):
+                lse_out[i:i + 1, :] = lse[:, i * LANES:(i + 1) * LANES]
 
         own_r = lse_own.at[t]
-        accs = r_phase(0, (0, 1, 2, 3), own_r, (zero,) * 4)
-        swap.wait_recv()
+        with scope("r_own"):
+            accs = r_phase(0, (0, 1, 2, 3), own_r, (zero,) * 4)
+        with scope("wait_swap"):
+            swap.wait_recv()
         oth_r = lse_oth.at[t]
-        acc_a = r_phase(1, (0, 1), oth_r, accs[:2])
+        with scope("r_oth_a"):
+            acc_a = r_phase(1, (0, 1), oth_r, accs[:2])
         counts = []
 
         def stats(lo):
@@ -227,13 +272,14 @@
             )
             s_buf[t, 2 * lo:2 * lo + 4] = out.reshape(4, kh, depth)
 
-        stats(0)
+        with scope("stats0"):
+            stats(0)
         scat = [
             send(s_buf.at[t, 2 * OPP], rs_in.at[t, 0], t, 5, right),
             send(s_buf.at[t, 2 * OPP + 1], rs_in.at[t, 1], t, 6, left),
-            send(s_buf.at[t, 2 * RIGHT + 1], rs_in.at[t, 2], t, 7, right),
         ]
-        acc_b = r_phase(1, (2, 3), oth_r, accs[2:])
+        with scope("r_oth_b"):
+            acc_b = r_phase(1, (2, 3), oth_r, accs[2:])
         for b, acc in enumerate(tuple(acc_a) + tuple(acc_b)):
             row = to_row(jnp.sum(acc, axis=1, keepdims=True))
             n_out[t, b, 0:1, :] = row
@@ -243,12 +289,20 @@
             send(n_out.at[t, RIGHT], n_in.at[t, 1], t, 9, right),
             send(n_out.at[t, LEFT], n_in.at[t, 2], t, 10, left),
         ]
-        stats(2)
+        with scope("stats2"):
+            stats(2)
+        with scope("wait_out"):
+            for c in scat:
+                c.wait_send()
+                pending[:] = [d for d in pending if d is not c]
+        scat.append(send(s_buf.at[t, 2 * RIGHT + 1], rs_in.at[t, 2], t, 7, right))
         scat.append(send(s_buf.at[t, 2 * LEFT], rs_in.at[t, 3], t, 11, left))
-        scat[0].wait_recv()
+        with scope("wait_s0"):
+            scat[0].wait_recv()
         acc_out[t, 0] = s_buf[t, 2 * RIGHT] + rs_in[t, 0]
         scat.append(send(acc_out.at[t, 0], rs_in.at[t, 4], t, 12, right))
-        scat[1].wait_recv()
+        with scope("wait_s1"):
+            scat[1].wait_recv()
         acc_out[t, 1] = s_buf[t, 2 * LEFT + 1] + rs_in[t, 1]
         scat.append(send(acc_out.at[t, 1], rs_in.at[t, 5], t, 13, left))
 
@@ -259,8 +313,9 @@
         n_col = to_col(n_row) + COUNT_EPS
         logw = jnp.log((n_row + PRIOR_ALPHA) / (n_total + k_total * PRIOR_ALPHA))
 
-        scat[3].wait_recv()
-        scat[4].wait_recv()
+        with scope("wait_s34"):
+            scat[3].wait_recv()
+            scat[4].wait_recv()
         mean_lo = (s_buf[t, 2 * OWN] + rs_in[t, 3] + rs_in[t, 4]) / n_col[:kh]
         if not last:
             nxt = mean_b.at[t + 1]
@@ -268,8 +323,9 @@
             mean_b[t + 1, OWN, 0:kh, :] = mean_lo.astype(jnp.bfloat16)
             mine_a, mine_b = nxt.at[OWN, a_rows], nxt.at[OWN, b_rows]
             g0 = send(mine_a, nxt.at[LEFT, a_rows], t, 14, right)
-            scat[2].wait_recv()
-            scat[5].wait_recv()
+            with scope("wait_s25"):
+                scat[2].wait_recv()
+                scat[5].wait_recv()
             mean_hi = (s_buf[t, 2 * OWN + 1] + rs_in[t, 2] + rs_in[t, 5]) / n_col[kh:]
             mean_b[t + 1, OWN, kh:kq, :] = mean_hi.astype(jnp.bfloat16)
             g3 = send(mine_b, nxt.at[RIGHT, b_rows], t, 17, left)
@@ -284,11 +340,14 @@
             g6 = send(src, prm.at[t + 1, LEFT], t, 20, right)
             g7 = send(src, prm.at[t + 1, RIGHT], t, 21, left)
             g8 = send(src, prm.at[t + 1, OPP], t, 22, opposite)
-            a_phase(t + 1, 1, (OWN,))
-            a_phase(t + 1, 0, (OWN,))
-            g0.wait_recv()
+            with scope("a_own"):
+                columns(t + 1, (OWN,))
+                a_phase(t + 1, tiles_of[1] + tiles_of[0], (OWN,))
+            with scope("wait_g0"):
+                g0.wait_recv()
             g2 = send(nxt.at[LEFT, a_rows], nxt.at[OPP, a_rows], t, 16, right)
-            g3.wait_recv()
+            with scope("wait_g3"):
+                g3.wait_recv()
             g5 = send(nxt.at[RIGHT, b_rows], nxt.at[OPP, b_rows], t, 19, left)
             gather = [g0, g1, g2, g3, g4, g5, g6, g7, g8]
         else:
@@ -302,8 +361,9 @@
 
             rows(0, False)[...] = mean_lo
             f0 = forward(0, False, 14, right)
-            scat[2].wait_recv()
-            scat[5].wait_recv()
+            with scope("wait_s25"):
+                scat[2].wait_recv()
+                scat[5].wait_recv()
             rows(0, True)[...] = (s_buf[t, 2 * OWN + 1] + rs_in[t, 2] + rs_in[t, 5]) / n_col[kh:]
             f3 = forward(0, True, 17, left)
             f1 = forward(0, True, 15, right)
@@ -314,30 +374,39 @@
             r7 = send(src, row_out.at[RIGHT], t, 21, left)
             r8 = send(src, row_out.at[OPP], t, 22, opposite)
             d2d = [forward(0, False, 23, partner), forward(0, True, 24, partner)]
-            f0.wait_recv()
+            with scope("wait_f0"):
+                f0.wait_recv()
             f2 = forward(3, False, 16, right)
             d2d.append(forward(3, False, 25, partner))
-            f3.wait_recv()
+            with scope("wait_f3"):
+                f3.wait_recv()
             f5 = forward(1, True, 19, left)
             d2d.append(forward(1, True, 26, partner))
             for c in (r6, r7, r8):
                 c.wait_recv()
             rows_copy = send(row_out, row_in, t, 30, partner)
-            f1.wait_recv()
+            with scope("wait_f1"):
+                f1.wait_recv()
             d2d.append(forward(3, True, 27, partner))
-            f4.wait_recv()
+            with scope("wait_f4"):
+                f4.wait_recv()
             d2d.append(forward(1, False, 28, partner))
-            f2.wait_recv()
+            with scope("wait_f2"):
+                f2.wait_recv()
             d2d.append(forward(2, False, 29, partner))
-            f5.wait_recv()
+            with scope("wait_f5"):
+                f5.wait_recv()
             d2d.append(forward(2, True, 32, partner))
-            rows_copy.wait_recv()
+            with scope("wait_rows"):
+                rows_copy.wait_recv()
             for b in range(4):
                 q = lax.rem(chip + SHIFT[b], n_chips)
                 logw_out[pl.ds(core * n_chips + q, 1), :] = row_out[b, 0:1, :]
                 logw_out[pl.ds((1 - core) * n_chips + q, 1), :] = row_in[b, 0:1, :]
-            for c in d2d:
-                c.wait_recv()
+            with scope("wait_d2d"):
+                for c in d2d:
+                    c.wait_recv()
+    with scope("drain"):
         drain()
 
 
@@ -358,18 +427,20 @@
             em_kernel, sweeps, n_loc * n_pts, k_loc * n_comp, n_chips, n_comp
         )
         vmem = pl.BlockSpec(memory_space=pltpu.VMEM)
-        anywhere = pl.BlockSpec(memory_space=pl.ANY)
+        hbm = pl.BlockSpec(memory_space=pltpu.HBM)
         V = pltpu.VMEM
         mean, logw, lse = pl.pallas_call(
             kernel,
             out_shape=(
                 jax.ShapeDtypeStruct((k_loc, depth), f32),
                 jax.ShapeDtypeStruct((n_pts, kq), f32),
-                jax.ShapeDtypeStruct((1, n_loc), f32),
+                jax.ShapeDtypeStruct((n_loc // LANES, LANES), f32),
             ),
-            in_specs=[pl.BlockSpec(memory_space=pltpu.SMEM), anywhere, anywhere, vmem],
+            in_specs=[hbm] * 4,
             out_specs=(vmem, vmem, vmem),
             scratch_shapes=[
+                pltpu.SMEM((sweeps,), f32),
+                V((n_pts, kq), f32),
                 V((2, n_loc, depth), bf16),
                 V((depth, 2 * n_loc), bf16),
                 V((1, 2 * n_loc), f32),
@@ -386,6 +457,10 @@
                 V((sweeps, n_comp - 1, 2, n_loc), f32),
                 V((sweeps, 1, n_loc), f32),
                 V((sweeps, 1, n_loc), f32),
+                V((4, kq, LANES), f32),
+                V((4, kq, LANES), f32),
+                V((half, min(256, n_loc)), f32),
+                V((half, min(256, n_loc)), f32),
                 V((sweeps, 8, kq // 2, depth), f32),
                 V((sweeps, 6, kq // 2, depth), f32),
                 V((sweeps, 2, kq // 2, depth), f32),
@@ -393,15 +468,15 @@
                 V((sweeps, 3, 8, kq), f32),
                 V((4, 8, kq), f32),
                 V((4, 8, kq), f32),
-                pltpu.SemaphoreType.DMA((sweeps, 33)),
-                pltpu.SemaphoreType.DMA((sweeps, 33)),
-                pltpu.SemaphoreType.DMA((5,)),
+                pltpu.SemaphoreType.DMA((sweeps, 40)),
+                pltpu.SemaphoreType.DMA((sweeps, 40)),
+                pltpu.SemaphoreType.DMA((7,)),
             ],
             compiler_params=pltpu.CompilerParams(
-                collective_id=0, has_side_effects=True, vmem_limit_bytes=60 * 1024 * 1024
+                collective_id=0, has_side_effects=True, vmem_limit_bytes=44 * 1024 * 1024
             ),
             name="em",
-        )(inv_temp, points, means, log_w.reshape(n_pts, kq))
+        )(*(pltpu.with_memory_space_constraint(v, pltpu.HBM) for v in (inv_temp, points, means, log_w.reshape(n_pts, kq))))
         return mean, logw.reshape(k_loc), lse.reshape(n_loc)
 
     comp_spec = P(("fit", "comp"))

time: 113 us -> 101 us (0.89)
  Pallas kernels: 107 us -> 98.2 us
  local copies, waits for them, and re-layouts: 4.29 us -> 2.51 us
    pallas_call x1, Pallas kernels: 107 us -> 98.2 us  [per_device(): pl.pallas_call(kernel, out_shape=(jax.ShapeDtypeStruct((k_loc, depth), f3...]
    unnamed x7 -> x3, local copies, waits for them, and re-layouts: 4.29 us -> 2.51 us
where the time goes in v2:
time: 101 us
  Pallas kernels  98.2 us (97%)
  local copies, waits for them, and re-layouts  2.51 us (2%)
    pallas_call x1, Pallas kernels, per_device(): pl.pallas_call(kernel, out_shape=(jax.ShapeDtypeStruct((k_loc, depth), f3...  98.2 us
    unnamed x3, local copies, waits for them, and re-layouts  2.51 us

profile of v2, /device:TPU:97, one launch (start us, length us, event | category | flops | bytes accessed | tf_op | source)
XLA Modules:
  0.0 101.4 jit_solution(10668537234589233477)
XLA Ops:
  0.6 98.2 %em.1 = (f32[1024,512]{1,0:T(8,128)S(1)}, f32[8,128]{1,0:T(8,128)S(1)}, f32[16,128]{1,0:T(8,128)S(1)}) custom-call(f32[3]{0:T(128)} %beta_hbm.1, bf16[2048,512]{1,0:T(8,128)(2,1)} %x_hbm.1, f32[1024,512]{1,0:T(8,128)} %mean_hbm.1, f32[8,128]{1,0:T(8,128)} %bitcast.5), custom_call_target="tpu_custom_call" | custom-call | tf_op jit(solution)/shard_map/em/pallas_call | solution.py:432
  98.9 1.3 %copy.10 = f32[1024,512]{1,0:T(8,128)} copy(f32[1024,512]{1,0:T(8,128)S(1)} %get-tuple-element.12) | data formatting | bytes 4194304
  100.2 0.6 copy.11
  100.8 0.6 copy.12

commit v3 on v2

v3 whole, which is shorter than its diff:
```python
import contextlib
import functools
import math

import jax
import jax.numpy as jnp
from jax import lax
from jax.experimental import pallas as pl
from jax.experimental.pallas import tpu as pltpu
from jax.sharding import PartitionSpec as P

PRIOR_ALPHA = 1e-3
COUNT_EPS = 1e-6
LOG2E = math.log2(math.e)
LN2 = math.log(2.0)
MESH = pl.DeviceIdType.MESH
scope = contextlib.nullcontext
CORES = 2
PARTS = 4
DIRECT = 0
LANES = 128

OPP, RIGHT, LEFT, OWN = range(4)
SHIFT = {OPP: 2, RIGHT: 1, LEFT: 3, OWN: 0}

PAIR, SWAP, COUNT, ROW, FINAL, XPART, PIECES = 0, 1, 2, 5, 9, 10, 14
FAR_A, FAR_B, NEAR_A, NEAR_B, SUM_A, SUM_B, OWN_A_RIGHT, OWN_B_RIGHT, OWN_A_LEFT, OWN_B_LEFT, ON_A, ON_B = range(
    PIECES, PIECES + 12 * PARTS, PARTS
)
ACROSS = PIECES + 12 * PARTS
SUMS_RIGHT, SUMS_LEFT, MEANS_RIGHT, MEANS_LEFT, X_OUT, FINAL_OUT, SINGLE = range(7)


def em_kernel(
    sweeps, n_total, k_total, n_chips, n_comp,
    beta_hbm, x_hbm, mean_hbm, logw_hbm,
    mean_out, logw_out, lse_out,
    beta_ref, logw_ref, x_all, xt, x_sq, e_buf, r_buf, mean_f, mean_b, prm, m_st, s_st, factor, pair_out, pair_in, glob_out, glob_in,
    lse_own, lse_oth, cols_c, raw_0, raw_1, n_acc, s_buf, rs_in, acc_out, n_out, n_in, row_out, row_in, send_sem, recv_sem, copy_sem,
):
    raw = (raw_0, raw_1)
    n_loc, depth = x_all.shape[1], x_all.shape[2]
    kq = mean_f.shape[1]
    kh, kp = kq // 2, kq // 2 // PARTS
    half = n_chips * kq

    p = lax.axis_index("pts")
    y = lax.axis_index("comp")
    chip = lax.div(p, CORES)
    core = p - chip * CORES
    partner = {"pts": chip * CORES + 1 - core}

    def x_peer(d):
        return {"pts": lax.rem(chip + d, n_chips) * CORES + core}

    right, left, opposite = x_peer(1), x_peer(n_chips - 1), x_peer(2)
    y_order = sorted(range(1, n_comp), key=lambda d: -min(d, n_comp - d))
    y_peers = [{"comp": lax.rem(y + d, n_comp)} for d in y_order]

    barrier = pltpu.get_barrier_semaphore()
    everyone = [partner, right, left, opposite] + y_peers
    for dev in everyone:
        pl.semaphore_signal(barrier, inc=1, device_id=dev, device_id_type=MESH)

    load_small = [
        pltpu.make_async_copy(logw_hbm, logw_ref, copy_sem.at[5]), pltpu.make_async_copy(beta_hbm, beta_ref, copy_sem.at[6])
    ]
    for c in load_small:
        c.start()
    load_mean = []
    for b in range(4):
        q = lax.rem(chip + SHIFT[b], n_chips)
        c = pltpu.make_async_copy(
            mean_hbm.at[pl.ds(pl.multiple_of(core * half + q * kq, kq), kq)], mean_f.at[b], copy_sem.at[b]
        )
        c.start()
        load_mean.append(c)

    load_x = pltpu.make_async_copy(x_hbm, x_all.at[0], copy_sem.at[4])
    load_x.start()

    pending = {}

    def send(src, dst, arrive, depart, dev, when=None):
        c = pltpu.make_async_remote_copy(
            src_ref=src, dst_ref=dst, send_sem=send_sem.at[depart], recv_sem=recv_sem.at[arrive],
            device_id=dev, device_id_type=MESH,
        )
        if depart >= SINGLE:
            if depart in pending:
                pending[depart].wait_send()
            pending[depart] = c
        if when is None:
            c.start()
        else:
            pl.when(when)(c.start)
        return c

    def wait_group(depart, ref):
        pltpu.make_async_remote_copy(
            src_ref=ref, dst_ref=ref, send_sem=send_sem.at[depart], recv_sem=recv_sem.at[PAIR],
            device_id=partner, device_id_type=MESH,
        ).wait_send()

    def wait_sums(t):
        wait_group(SUMS_RIGHT, rs_in.at[t, pl.ds(0, 3)])
        wait_group(SUMS_LEFT, rs_in.at[t, pl.ds(0, 3)])

    def wait_means(t):
        ref = mean_b.at[t + 1, pl.ds(0, 3), pl.ds(0, kh)] if t < sweeps - 1 else mean_out.at[pl.ds(0, 3 * kh)]
        wait_group(MEANS_RIGHT, ref)
        wait_group(MEANS_LEFT, ref)

    eye = lax.broadcasted_iota(jnp.int32, (kq, kq), 0) == lax.broadcasted_iota(jnp.int32, (kq, kq), 1)

    def to_col(row):
        return jnp.sum(jnp.where(eye, jnp.broadcast_to(row, (kq, kq)), 0.0), axis=1, keepdims=True)

    def to_row(col):
        return jnp.sum(jnp.where(eye, jnp.broadcast_to(col, (kq, kq)), 0.0), axis=0, keepdims=True)

    with scope("loads"):
        for c in load_small:
            c.wait()
    tr = min(512, n_loc)
    n_tr = n_loc // tr
    with scope("barrier"):
        pl.semaphore_wait(barrier, len(everyone))
    x_rows = [pl.ds(c * tr, tr) for c in range(n_tr)]
    x_copies = [send(x_hbm.at[r], x_all.at[1, r], XPART + c, X_OUT, partner) for c, r in enumerate(x_rows)]
    with scope("meanprep"):
        for b in range(4):
            load_mean[b].wait()
            mf = mean_f[b]
            mean_b[0, b] = mf.astype(jnp.bfloat16)
            q = lax.rem(chip + SHIFT[b], n_chips)
            prm[0, b, 0:1, :] = logw_ref[pl.ds(core * n_chips + q, 1), :]
            prm[0, b, 1:2, :] = to_row(jnp.sum(mf * mf, axis=1, keepdims=True))

    def prepare(h, c):
        cols = slice(h * n_loc + c * tr, h * n_loc + (c + 1) * tr)
        blk = x_all[h, c * tr:(c + 1) * tr, :].T
        xt[:, cols] = blk
        if h == 0:
            f = blk.astype(jnp.float32)
            x_sq[:, cols] = jnp.sum(f * f, axis=0, keepdims=True)

    tile = min(256, n_loc)

    def columns(t, blocks):
        for b in blocks:
            row = (prm[t, b, 0:1, :] - beta_ref[t] * prm[t, b, 1:2, :]) * LOG2E
            cols_c[b] = jnp.broadcast_to(to_col(row), (kq, LANES))

    def a_phase(t, tiles, blocks):
        slope = beta_ref[t] * (2.0 * LOG2E)
        lo, nb = blocks[0], len(blocks)
        means = mean_b.at[t, lo:lo + nb]

        def product(u):
            cols = slice(tiles[u] * tile, (tiles[u] + 1) * tile)
            raw[u % 2][0:nb * kq] = jnp.dot(
                means[...].reshape(nb * kq, depth), xt[:, cols], preferred_element_type=jnp.float32
            )

        product(0)
        for u in range(len(tiles)):
            if u + 1 < len(tiles):
                product(u + 1)
            for v in range(tile // LANES):
                at = tiles[u] * tile + v * LANES
                cols = slice(at, at + LANES)
                for i, b in enumerate(blocks):
                    a = raw[u % 2][i * kq:(i + 1) * kq, v * LANES:(v + 1) * LANES]
                    logit = a * slope + cols_c[b]
                    m = jnp.max(logit, axis=0, keepdims=True)
                    e = jnp.exp2(logit - m)
                    e_buf[b * kq:(b + 1) * kq, cols] = e
                    m_st[b:b + 1, cols] = m
                    s_st[b:b + 1, cols] = jnp.sum(e, axis=0, keepdims=True)

    per_half = n_loc // tile
    tiles_of = [list(range(per_half)), list(range(per_half, 2 * per_half))]

    def local_pair(h):
        cols = pl.ds(h * n_loc, n_loc)
        ms = [m_st[b:b + 1, cols] for b in range(4)]
        m = jnp.maximum(jnp.maximum(ms[0], ms[1]), jnp.maximum(ms[2], ms[3]))
        s = sum(s_st[b:b + 1, cols] * jnp.exp2(ms[b] - m) for b in range(4))
        return m, s

    def r_phase(h, blocks, lse):
        half_cols = slice(h * n_loc, (h + 1) * n_loc)
        if 0 in blocks:
            factor[:, half_cols] = jnp.exp2(m_st[:, half_cols] - lse[...])
        accs = [jnp.zeros((kq, LANES), jnp.float32) for _ in blocks]
        for c in range(n_loc // LANES):
            cols = slice(h * n_loc + c * LANES, h * n_loc + (c + 1) * LANES)
            for i, b in enumerate(blocks):
                r = e_buf[b * kq:(b + 1) * kq, cols] * factor[b:b + 1, cols]
                r_buf[b * kq:(b + 1) * kq, cols] = r.astype(jnp.bfloat16)
                accs[i] = accs[i] + r
        for i, b in enumerate(blocks):
            n_acc[h, b] = accs[i]

    def stats(h, lo):
        out = jnp.dot(
            r_buf[lo * kq:(lo + 2) * kq, h * n_loc:(h + 1) * n_loc], x_all[h], preferred_element_type=jnp.float32
        ).reshape(4, kh, depth)
        if h == 0:
            s_buf[t, 2 * lo:2 * lo + 4] = out
        else:
            s_buf[t, 2 * lo:2 * lo + 4] += out

    for t in range(sweeps):
        last = t == sweeps - 1
        if t == 0:
            columns(0, range(4))
            with scope("loadx"):
                load_x.wait()
            with scope("prep0"):
                for c in range(n_tr):
                    prepare(0, c)
            with scope("a00"):
                a_phase(t, tiles_of[0], range(4))
            per_tr = tr // tile
            for c in range(n_tr):
                with scope("xwait"):
                    x_copies[c].wait_recv()
                with scope("prep1"):
                    prepare(1, c)
                with scope("a01"):
                    a_phase(t, tiles_of[1][c * per_tr:(c + 1) * per_tr], range(4))
        else:
            with scope("wait_near"):
                for c in b_right + a_left + rows[:2]:
                    c.wait_recv()
            with scope("a_right"):
                columns(t, (RIGHT, LEFT))
                a_phase(t, tiles_of[1] + tiles_of[0], (RIGHT, LEFT))
            with scope("wait_opp"):
                for c in a_on + b_on + rows[2:]:
                    c.wait_recv()
            with scope("a_opp1"):
                columns(t, (OPP,))
                a_phase(t, tiles_of[1], (OPP,))
        m, s = local_pair(1)
        pair_out[t, 0:1, :] = m
        pair_out[t, 1:2, :] = s
        pair = send(pair_out.at[t], pair_in.at[t], PAIR, SINGLE, partner)
        if t > 0:
            with scope("a_opp0"):
                a_phase(t, tiles_of[0], (OPP,))
        m, s = local_pair(0)
        with scope("wait_pair"):
            pair.wait_recv()
        m1, s1 = pair_in[t, 0:1, :], pair_in[t, 1:2, :]
        top = jnp.maximum(m, m1)
        s = s * jnp.exp2(m - top) + s1 * jnp.exp2(m1 - top)
        glob_out[t, 0:1, :] = top
        glob_out[t, 1:2, :] = s
        across = [
            send(glob_out.at[t], glob_in.at[t, d], ACROSS + t * (n_comp - 1) + d, SINGLE + 9 + d, y_peers[d])
            for d in range(n_comp - 1)
        ]
        tops, sums = [top], [s]
        for d in reversed(range(n_comp - 1)):
            with scope("wait_y"):
                across[d].wait_recv()
            tops.append(glob_in[t, d, 0:1, :])
            sums.append(glob_in[t, d, 1:2, :])
        top = functools.reduce(jnp.maximum, tops)
        total = sum(v * jnp.exp2(w - top) for v, w in zip(sums, tops))
        lse2 = top + jnp.log(total) * LOG2E
        lse_own[t] = lse2
        swap = send(lse_own.at[t], lse_oth.at[t], SWAP, SINGLE + 1, partner)
        if last:
            lse = lse2 * LN2 - beta_ref[t] * x_sq[...]
            for i in range(n_loc // LANES):
                lse_out[i:i + 1, :] = lse[:, i * LANES:(i + 1) * LANES]

        own_r, oth_r = lse_own.at[t], lse_oth.at[t]
        with scope("r_own_a"):
            r_phase(0, (0, 1), own_r)
        with scope("stats0"):
            stats(0, 0)
        with scope("wait_swap"):
            swap.wait_recv()
        with scope("r_oth_a"):
            r_phase(1, (0, 1), oth_r)
        with scope("stats1"):
            stats(1, 0)

        parts = [pl.ds(i * kp, kp) for i in range(PARTS)]

        def s_piece(b, half_b, i):
            return s_buf.at[t, 2 * b + half_b, parts[i]]

        def in_piece(slot, i):
            return rs_in.at[t, slot, parts[i]]

        def near_b_send(i, when=None):
            return send(s_piece(RIGHT, 1, i), in_piece(2, i), NEAR_B + i, SUMS_RIGHT, right, when)

        def near_a_send(i):
            return send(s_piece(LEFT, 0, i), in_piece(3, i), NEAR_A + i, SUMS_LEFT, left)

        def first_sends(when):
            a, b = [], []
            for i in range(PARTS):
                a.append(send(s_piece(OPP, 0, i), in_piece(0, i), FAR_A + i, SUMS_RIGHT, right, when))
                b.append(send(s_piece(OPP, 1, i), in_piece(1, i), FAR_B + i, SUMS_LEFT, left, when))
            return a, b, [near_b_send(i, when) for i in range(2)]

        if t > 0:
            wait_sums(t - 1)
        far_a, far_b, near_b = first_sends(core == 0)
        with scope("r_23"):
            r_phase(0, (2, 3), own_r)
            r_phase(1, (2, 3), oth_r)
        counts = []
        for b in range(4):
            row = to_row(jnp.sum(n_acc[0, b] + n_acc[1, b], axis=1, keepdims=True))
            n_out[t, b, 0:1, :] = row
            counts.append(row)
        n_copies = [
            send(n_out.at[t, b], n_in.at[t, d], COUNT + d, SINGLE + 2 + d, dev)
            for d, (b, dev) in enumerate(((OPP, opposite), (RIGHT, right), (LEFT, left)))
        ]
        with scope("stats2"):
            stats(0, 2)
            stats(1, 2)
        first_sends(core == 1)
        near_a = [near_a_send(i) for i in range(2)]
        sum_a, sum_b = [], []
        for i in range(PARTS):
            with scope("wait_far_a"):
                far_a[i].wait_recv()
            acc_out[t, 0, parts[i]] = s_buf[t, 2 * RIGHT, parts[i]] + rs_in[t, 0, parts[i]]
            sum_a.append(send(acc_out.at[t, 0, parts[i]], in_piece(4, i), SUM_A + i, SUMS_RIGHT, right))
            if i + 2 < PARTS:
                near_b.append(near_b_send(i + 2))
            with scope("wait_far_b"):
                far_b[i].wait_recv()
            acc_out[t, 1, parts[i]] = s_buf[t, 2 * LEFT + 1, parts[i]] + rs_in[t, 1, parts[i]]
            sum_b.append(send(acc_out.at[t, 1, parts[i]], in_piece(5, i), SUM_B + i, SUMS_LEFT, left))
            if i + 2 < PARTS:
                near_a.append(near_a_send(i + 2))

        n_row = counts[OWN]
        for d in range(3):
            with scope("wait_n"):
                n_copies[d].wait_recv()
            n_row = n_row + n_in[t, d, 0:1, :]
        n_col = to_col(n_row) + COUNT_EPS
        logw = jnp.log((n_row + PRIOR_ALPHA) / (n_total + k_total * PRIOR_ALPHA))

        def m_piece(b, half_b, i):
            at = half_b * kh + i * kp
            if not last:
                return mean_b.at[t + 1, b, pl.ds(at, kp)]
            q = lax.rem(chip + SHIFT[b], n_chips)
            return mean_out.at[pl.ds(pl.multiple_of(core * half + q * kq + at, kp), kp)]

        def m_send(b, there, half_b, i, arrive, dev):
            depart = MEANS_LEFT if arrive >= OWN_A_LEFT and not ON_A <= arrive < ON_B else MEANS_RIGHT
            return send(m_piece(b, half_b, i), m_piece(b if last else there, half_b, i), arrive, depart, dev)

        def swap_piece(b, half_b, i):
            if last:
                send(m_piece(b, half_b, i), m_piece(b, half_b, i), FINAL, FINAL_OUT, partner)

        if t > 0:
            wait_means(t - 1)
        sq = {}
        a_right, b_right, a_left, b_left, a_on, b_on, a_direct, b_direct = ([] for _ in range(8))
        for i in range(PARTS):
            for half_b, far, near, slots in ((0, sum_a, near_a, (3, 4)), (1, sum_b, near_b, (2, 5))):
                with scope("wait_sum"):
                    near[i].wait_recv()
                    far[i].wait_recv()
                at = half_b * kh + i * kp
                mean = (
                    s_buf[t, 2 * OWN + half_b, parts[i]] + rs_in[t, slots[0], parts[i]] + rs_in[t, slots[1], parts[i]]
                ) / n_col[at:at + kp]
                m_piece(OWN, half_b, i)[...] = mean if last else mean.astype(jnp.bfloat16)
                sq[half_b, i] = jnp.sum(mean * mean, axis=1, keepdims=True)
                if half_b == 0:
                    a_right.append(m_send(OWN, LEFT, 0, i, OWN_A_RIGHT + i, right))
                else:
                    b_left.append(m_send(OWN, RIGHT, 1, i, OWN_B_LEFT + i, left))
            b_right.append(m_send(OWN, LEFT, 1, i, OWN_B_RIGHT + i, right))
            a_left.append(m_send(OWN, RIGHT, 0, i, OWN_A_LEFT + i, left))
            if i >= PARTS - DIRECT:
                a_direct.append(m_send(OWN, OPP, 0, i, ON_A + i, opposite))
                b_direct.append(m_send(OWN, OPP, 1, i, ON_B + i, opposite))
            swap_piece(OWN, 0, i)
            swap_piece(OWN, 1, i)

        own_row, to_rows = (row_out.at[OWN], row_out) if last else (prm.at[t + 1, OWN], prm.at[t + 1])
        own_row[0:1, :] = logw
        if not last:
            col = jnp.concatenate([sq[h, i] for h in range(2) for i in range(PARTS)], axis=0)
            own_row[1:2, :] = to_row(col)
        rows = [
            send(own_row, to_rows.at[LEFT], ROW, SINGLE + 5, right),
            send(own_row, to_rows.at[RIGHT], ROW + 1, SINGLE + 6, left),
            send(own_row, to_rows.at[OPP], ROW + 2, SINGLE + 7, opposite),
        ]
        if not last:
            with scope("a_own"):
                columns(t + 1, (OWN,))
                a_phase(t + 1, tiles_of[1] + tiles_of[0], (OWN,))
        for i in range(PARTS):
            with scope("wait_on_a"):
                a_right[i].wait_recv()
            if i < PARTS - DIRECT:
                a_on.append(m_send(LEFT, OPP, 0, i, ON_A + i, right))
            with scope("wait_on_b"):
                b_left[i].wait_recv()
            if i < PARTS - DIRECT:
                b_on.append(m_send(RIGHT, OPP, 1, i, ON_B + i, left))
            swap_piece(LEFT, 0, i)
            swap_piece(RIGHT, 1, i)
        a_on += a_direct
        b_on += b_direct
        if last:
            with scope("wait_rows"):
                for c in rows:
                    c.wait_recv()
            rows_copy = send(row_out, row_in, ROW + 3, SINGLE + 8, partner)
            for i in range(PARTS):
                with scope("wait_bl"):
                    b_right[i].wait_recv()
                swap_piece(LEFT, 1, i)
                with scope("wait_ar"):
                    a_left[i].wait_recv()
                swap_piece(RIGHT, 0, i)
            for i in range(PARTS):
                with scope("wait_oa"):
                    a_on[i].wait_recv()
                swap_piece(OPP, 0, i)
                with scope("wait_ob"):
                    b_on[i].wait_recv()
                swap_piece(OPP, 1, i)
            with scope("wait_d2dr"):
                rows_copy.wait_recv()
            for b in range(4):
                q = lax.rem(chip + SHIFT[b], n_chips)
                logw_out[pl.ds(core * n_chips + q, 1), :] = row_out[b, 0:1, :]
                logw_out[pl.ds((1 - core) * n_chips + q, 1), :] = row_in[b, 0:1, :]
            with scope("wait_d2d"):
                theirs = mean_out.at[pl.ds(pl.multiple_of((1 - core) * half, half), half)]
                pltpu.make_async_remote_copy(
                    src_ref=theirs, dst_ref=theirs, send_sem=send_sem.at[FINAL_OUT], recv_sem=recv_sem.at[FINAL],
                    device_id=partner, device_id_type=MESH,
                ).wait_recv()
    with scope("drain"):
        for c in pending.values():
            c.wait_send()
        wait_group(X_OUT, x_all.at[1])
        wait_sums(sweeps - 1)
        wait_means(sweeps - 1)
        wait_group(FINAL_OUT, mean_out.at[pl.ds(0, half)])


def solution(mesh):
    n_pts, n_comp = mesh.shape["pts"], mesh.shape["comp"]
    n_chips = n_pts // CORES

    def per_device(points, means, log_w, inv_temp):
        n_loc, depth = points.shape
        k_loc = means.shape[0]
        kq = k_loc // n_pts
        half = n_chips * kq
        sweeps = inv_temp.shape[0]
        if n_chips != 4 or kq != LANES:
            raise ValueError("unsupported shape")
        f32, bf16 = jnp.float32, jnp.bfloat16
        kernel = functools.partial(
            em_kernel, sweeps, n_loc * n_pts, k_loc * n_comp, n_chips, n_comp
        )
        vmem = pl.BlockSpec(memory_space=pltpu.VMEM)
        hbm = pl.BlockSpec(memory_space=pltpu.HBM)
        V = pltpu.VMEM
        mean, logw, lse = pl.pallas_call(
            kernel,
            out_shape=(
                jax.ShapeDtypeStruct((k_loc, depth), f32),
                jax.ShapeDtypeStruct((n_pts, kq), f32),
                jax.ShapeDtypeStruct((n_loc // LANES, LANES), f32),
            ),
            in_specs=[hbm] * 4,
            out_specs=(vmem, vmem, vmem),
            scratch_shapes=[
                pltpu.SMEM((sweeps,), f32),
                V((n_pts, kq), f32),
                V((2, n_loc, depth), bf16),
                V((depth, 2 * n_loc), bf16),
                V((1, n_loc), f32),
                V((half, 2 * n_loc), f32),
                V((half, 2 * n_loc), bf16),
                V((4, kq, depth), f32),
                V((sweeps, 4, kq, depth), bf16),
                V((sweeps, 4, 8, kq), f32),
                V((4, 2 * n_loc), f32),
                V((4, 2 * n_loc), f32),
                V((4, 2 * n_loc), f32),
                V((sweeps, 2, n_loc), f32),
                V((sweeps, 2, n_loc), f32),
                V((sweeps, 2, n_loc), f32),
                V((sweeps, n_comp - 1, 2, n_loc), f32),
                V((sweeps, 1, n_loc), f32),
                V((sweeps, 1, n_loc), f32),
                V((4, kq, LANES), f32),
                V((half, min(256, n_loc)), f32),
                V((half, min(256, n_loc)), f32),
                V((2, 4, kq, LANES), f32),
                V((sweeps, 8, kq // 2, depth), f32),
                V((sweeps, 6, kq // 2, depth), f32),
                V((sweeps, 2, kq // 2, depth), f32),
                V((sweeps, 4, 8, kq), f32),
                V((sweeps, 3, 8, kq), f32),
                V((4, 8, kq), f32),
                V((4, 8, kq), f32),
                pltpu.SemaphoreType.DMA((SINGLE + 8 + n_comp,)),
                pltpu.SemaphoreType.DMA((ACROSS + sweeps * (n_comp - 1),)),
                pltpu.SemaphoreType.DMA((7,)),
            ],
            compiler_params=pltpu.CompilerParams(
                collective_id=0, has_side_effects=True, vmem_limit_bytes=44 * 1024 * 1024
            ),
            name="em",
        )(*(pltpu.with_memory_space_constraint(v, pltpu.HBM) for v in (inv_temp, points, means, log_w.reshape(n_pts, kq))))
        return mean, logw.reshape(k_loc), lse.reshape(n_loc)

    comp_spec = P(("fit", "comp"))
    return jax.shard_map(
        per_device,
        mesh=mesh,
        in_specs=(P(("fit", "pts"), None), P(("fit", "comp"), None), comp_spec, P()),
        out_specs=(P(("fit", "comp"), None), comp_spec, P(("fit", "pts"))),
        check_vma=False,
    )
```

time: 101 us -> 91.1 us (0.902)
  Pallas kernels: 98.2 us -> 87.8 us
    pallas_call x1, Pallas kernels: 98.2 us -> 87.8 us  [per_device(): pl.pallas_call(kernel, out_shape=(jax.ShapeDtypeStruct((k_loc, depth), f3...]
where the time goes in v3:
time: 91.1 us; the launch traced here: 91 us
  Pallas kernels  87.8 us (96%)
  local copies, waits for them, and re-layouts  2.51 us (3%)
    pallas_call x1, Pallas kernels, per_device(): pl.pallas_call(kernel, out_shape=(jax.ShapeDtypeStruct((k_loc, depth), f3...  87.8 us
    unnamed x3, local copies, waits for them, and re-layouts  2.51 us

profile of v3, /device:TPU:97, one launch (start us, length us, event | category | flops | bytes accessed | tf_op | source)
XLA Modules:
  0.0 91.0 jit_solution(6681607797666873113)
XLA Ops:
  0.6 87.8 %em.1 = (f32[1024,512]{1,0:T(8,128)S(1)}, f32[8,128]{1,0:T(8,128)S(1)}, f32[16,128]{1,0:T(8,128)S(1)}) custom-call(f32[3]{0:T(128)} %beta_hbm.1, bf16[2048,512]{1,0:T(8,128)(2,1)} %x_hbm.1, f32[1024,512]{1,0:T(8,128)} %mean_hbm.1, f32[8,128]{1,0:T(8,128)} %bitcast.5), custom_call_target="tpu_custom_call" | custom-call | tf_op jit(solution)/shard_map/em/pallas_call | solution.py:486
  88.4 1.3 %copy.10 = f32[1024,512]{1,0:T(8,128)} copy(f32[1024,512]{1,0:T(8,128)S(1)} %get-tuple-element.12) | data formatting | bytes 4194304
  89.8 0.6 copy.11
  90.4 0.6 copy.12

commit v4 on v3

--- a/solution.py
+++ b/solution.py
@@ -62,8 +62,13 @@
     for dev in everyone:
         pl.semaphore_signal(barrier, inc=1, device_id=dev, device_id_type=MESH)
 
+    tr = min(512, n_loc // 2)
+    n_tr = n_loc // tr
+    x_rows = [pl.ds(c * tr, tr) for c in range(n_tr)]
+    load_x = [pltpu.make_async_copy(x_hbm.at[r], x_all.at[0, r], copy_sem.at[6 + c]) for c, r in enumerate(x_rows)]
+    load_x[0].start()
     load_small = [
-        pltpu.make_async_copy(logw_hbm, logw_ref, copy_sem.at[5]), pltpu.make_async_copy(beta_hbm, beta_ref, copy_sem.at[6])
+        pltpu.make_async_copy(logw_hbm, logw_ref, copy_sem.at[4]), pltpu.make_async_copy(beta_hbm, beta_ref, copy_sem.at[5])
     ]
     for c in load_small:
         c.start()
@@ -76,8 +81,8 @@
         c.start()
         load_mean.append(c)
 
-    load_x = pltpu.make_async_copy(x_hbm, x_all.at[0], copy_sem.at[4])
-    load_x.start()
+    for c in load_x[1:]:
+        c.start()
 
     pending = {}
 
@@ -119,15 +124,12 @@
     def to_row(col):
         return jnp.sum(jnp.where(eye, jnp.broadcast_to(col, (kq, kq)), 0.0), axis=0, keepdims=True)
 
+    with scope("barrier"):
+        pl.semaphore_wait(barrier, len(everyone))
+    x_copies = [send(x_hbm.at[r], x_all.at[1, r], XPART + c, X_OUT, partner) for c, r in enumerate(x_rows)]
     with scope("loads"):
         for c in load_small:
             c.wait()
-    tr = min(512, n_loc)
-    n_tr = n_loc // tr
-    with scope("barrier"):
-        pl.semaphore_wait(barrier, len(everyone))
-    x_rows = [pl.ds(c * tr, tr) for c in range(n_tr)]
-    x_copies = [send(x_hbm.at[r], x_all.at[1, r], XPART + c, X_OUT, partner) for c, r in enumerate(x_rows)]
     with scope("meanprep"):
         for b in range(4):
             load_mean[b].wait()
@@ -137,22 +139,22 @@
             prm[0, b, 0:1, :] = logw_ref[pl.ds(core * n_chips + q, 1), :]
             prm[0, b, 1:2, :] = to_row(jnp.sum(mf * mf, axis=1, keepdims=True))
 
-    def prepare(h, c):
-        cols = slice(h * n_loc + c * tr, h * n_loc + (c + 1) * tr)
-        blk = x_all[h, c * tr:(c + 1) * tr, :].T
-        xt[:, cols] = blk
+    tile = min(256, n_loc // 2)
+
+    def prepare(u):
+        h, at = divmod(u * tile, n_loc)
+        blk = x_all[h, at:at + tile, :].T
+        xt[:, u * tile:(u + 1) * tile] = blk
         if h == 0:
             f = blk.astype(jnp.float32)
-            x_sq[:, cols] = jnp.sum(f * f, axis=0, keepdims=True)
-
-    tile = min(256, n_loc)
+            x_sq[:, at:at + tile] = jnp.sum(f * f, axis=0, keepdims=True)
 
     def columns(t, blocks):
         for b in blocks:
             row = (prm[t, b, 0:1, :] - beta_ref[t] * prm[t, b, 1:2, :]) * LOG2E
             cols_c[b] = jnp.broadcast_to(to_col(row), (kq, LANES))
 
-    def a_phase(t, tiles, blocks):
+    def a_phase(t, tiles, blocks, ahead=None):
         slope = beta_ref[t] * (2.0 * LOG2E)
         lo, nb = blocks[0], len(blocks)
         means = mean_b.at[t, lo:lo + nb]
@@ -163,10 +165,15 @@
                 means[...].reshape(nb * kq, depth), xt[:, cols], preferred_element_type=jnp.float32
             )
 
+        if ahead is not None:
+            ahead(tiles[0])
+            ahead(tiles[1])
         product(0)
         for u in range(len(tiles)):
             if u + 1 < len(tiles):
                 product(u + 1)
+            if ahead is not None and u + 2 < len(tiles):
+                ahead(tiles[u + 2])
             for v in range(tile // LANES):
                 at = tiles[u] * tile + v * LANES
                 cols = slice(at, at + LANES)
@@ -189,25 +196,29 @@
         s = sum(s_st[b:b + 1, cols] * jnp.exp2(ms[b] - m) for b in range(4))
         return m, s
 
-    def r_phase(h, blocks, lse):
-        half_cols = slice(h * n_loc, (h + 1) * n_loc)
-        if 0 in blocks:
-            factor[:, half_cols] = jnp.exp2(m_st[:, half_cols] - lse[...])
-        accs = [jnp.zeros((kq, LANES), jnp.float32) for _ in blocks]
-        for c in range(n_loc // LANES):
-            cols = slice(h * n_loc + c * LANES, h * n_loc + (c + 1) * LANES)
-            for i, b in enumerate(blocks):
+    chunk = n_loc // 2
+
+    def factors(h, lse):
+        cols = slice(h * n_loc, (h + 1) * n_loc)
+        factor[:, cols] = jnp.exp2(m_st[:, cols] - lse[...])
+
+    def r_phase(h, lo, c):
+        for b in (lo, lo + 1):
+            acc = jnp.zeros((kq, LANES), jnp.float32)
+            for at in range(h * n_loc + c * chunk, h * n_loc + (c + 1) * chunk, LANES):
+                cols = slice(at, at + LANES)
                 r = e_buf[b * kq:(b + 1) * kq, cols] * factor[b:b + 1, cols]
                 r_buf[b * kq:(b + 1) * kq, cols] = r.astype(jnp.bfloat16)
-                accs[i] = accs[i] + r
-        for i, b in enumerate(blocks):
-            n_acc[h, b] = accs[i]
-
-    def stats(h, lo):
+                acc = acc + r
+            n_acc[2 * h + c, b] = acc
+
+    def stats(h, lo, c):
+        at = h * n_loc + c * chunk
         out = jnp.dot(
-            r_buf[lo * kq:(lo + 2) * kq, h * n_loc:(h + 1) * n_loc], x_all[h], preferred_element_type=jnp.float32
+            r_buf[lo * kq:(lo + 2) * kq, at:at + chunk], x_all[h, c * chunk:(c + 1) * chunk],
+            preferred_element_type=jnp.float32,
         ).reshape(4, kh, depth)
-        if h == 0:
+        if h == 0 and c == 0:
             s_buf[t, 2 * lo:2 * lo + 4] = out
         else:
             s_buf[t, 2 * lo:2 * lo + 4] += out
@@ -217,20 +228,16 @@
         if t == 0:
             columns(0, range(4))
             with scope("loadx"):
-                load_x.wait()
-            with scope("prep0"):
-                for c in range(n_tr):
-                    prepare(0, c)
+                for c in load_x:
+                    c.wait()
             with scope("a00"):
-                a_phase(t, tiles_of[0], range(4))
-            per_tr = tr // tile
-            for c in range(n_tr):
+                a_phase(t, tiles_of[0], range(4), prepare)
+            for g in range(2):
                 with scope("xwait"):
-                    x_copies[c].wait_recv()
-                with scope("prep1"):
-                    prepare(1, c)
+                    for c in x_copies[g * n_tr // 2:(g + 1) * n_tr // 2]:
+                        c.wait_recv()
                 with scope("a01"):
-                    a_phase(t, tiles_of[1][c * per_tr:(c + 1) * per_tr], range(4))
+                    a_phase(t, tiles_of[1][g * per_half // 2:(g + 1) * per_half // 2], range(4), prepare)
         else:
             with scope("wait_near"):
                 for c in b_right + a_left + rows[:2]:
@@ -279,17 +286,20 @@
             for i in range(n_loc // LANES):
                 lse_out[i:i + 1, :] = lse[:, i * LANES:(i + 1) * LANES]
 
-        own_r, oth_r = lse_own.at[t], lse_oth.at[t]
-        with scope("r_own_a"):
-            r_phase(0, (0, 1), own_r)
-        with scope("stats0"):
-            stats(0, 0)
+        with scope("rs_own"):
+            factors(0, lse_own.at[t])
+            r_phase(0, 0, 0)
+            r_phase(0, 0, 1)
+            stats(0, 0, 0)
         with scope("wait_swap"):
             swap.wait_recv()
-        with scope("r_oth_a"):
-            r_phase(1, (0, 1), oth_r)
         with scope("stats1"):
-            stats(1, 0)
+            factors(1, lse_oth.at[t])
+            r_phase(1, 0, 0)
+            stats(0, 0, 1)
+            r_phase(1, 0, 1)
+            stats(1, 0, 0)
+            stats(1, 0, 1)
 
         parts = [pl.ds(i * kp, kp) for i in range(PARTS)]
 
@@ -316,11 +326,12 @@
             wait_sums(t - 1)
         far_a, far_b, near_b = first_sends(core == 0)
         with scope("r_23"):
-            r_phase(0, (2, 3), own_r)
-            r_phase(1, (2, 3), oth_r)
+            for h in range(2):
+                for c in range(2):
+                    r_phase(h, 2, c)
         counts = []
         for b in range(4):
-            row = to_row(jnp.sum(n_acc[0, b] + n_acc[1, b], axis=1, keepdims=True))
+            row = to_row(jnp.sum((n_acc[0, b] + n_acc[1, b]) + (n_acc[2, b] + n_acc[3, b]), axis=1, keepdims=True))
             n_out[t, b, 0:1, :] = row
             counts.append(row)
         n_copies = [
@@ -328,8 +339,9 @@
             for d, (b, dev) in enumerate(((OPP, opposite), (RIGHT, right), (LEFT, left)))
         ]
         with scope("stats2"):
-            stats(0, 2)
-            stats(1, 2)
+            for h in range(2):
+                for c in range(2):
+                    stats(h, 2, c)
         first_sends(core == 1)
         near_a = [near_a_send(i) for i in range(2)]
         sum_a, sum_b = [], []
@@ -370,8 +382,20 @@
             if last:
                 send(m_piece(b, half_b, i), m_piece(b, half_b, i), FINAL, FINAL_OUT, partner)
 
+        rows = []
+
+        def send_rows(mean_sq=None):
+            own_row, to_rows = (row_out.at[OWN], row_out) if last else (prm.at[t + 1, OWN], prm.at[t + 1])
+            own_row[0:1, :] = logw
+            if mean_sq is not None:
+                own_row[1:2, :] = mean_sq
+            for d, (b, dev) in enumerate(((LEFT, right), (RIGHT, left), (OPP, opposite))):
+                rows.append(send(own_row, to_rows.at[b], ROW + d, SINGLE + 5 + d, dev))
+
         if t > 0:
             wait_means(t - 1)
+        if last:
+            send_rows()
         sq = {}
         a_right, b_right, a_left, b_left, a_on, b_on, a_direct, b_direct = ([] for _ in range(8))
         for i in range(PARTS):
@@ -397,16 +421,8 @@
             swap_piece(OWN, 0, i)
             swap_piece(OWN, 1, i)
 
-        own_row, to_rows = (row_out.at[OWN], row_out) if last else (prm.at[t + 1, OWN], prm.at[t + 1])
-        own_row[0:1, :] = logw
         if not last:
-            col = jnp.concatenate([sq[h, i] for h in range(2) for i in range(PARTS)], axis=0)
-            own_row[1:2, :] = to_row(col)
-        rows = [
-            send(own_row, to_rows.at[LEFT], ROW, SINGLE + 5, right),
-            send(own_row, to_rows.at[RIGHT], ROW + 1, SINGLE + 6, left),
-            send(own_row, to_rows.at[OPP], ROW + 2, SINGLE + 7, opposite),
-        ]
+            send_rows(to_row(jnp.concatenate([sq[h, i] for h in range(2) for i in range(PARTS)], axis=0)))
         if not last:
             with scope("a_own"):
                 columns(t + 1, (OWN,))
@@ -464,6 +480,17 @@
         wait_group(FINAL_OUT, mean_out.at[pl.ds(0, half)])
 
 
+def pass_kernel(mean_in, logw_in, lse_in, mean_out, logw_out, lse_out, sem):
+    copies = [
+        pltpu.make_async_copy(src, dst, sem.at[i])
+        for i, (src, dst) in enumerate(((mean_in, mean_out), (logw_in, logw_out), (lse_in, lse_out)))
+    ]
+    for c in copies:
+        c.start()
+    for c in copies:
+        c.wait()
+
+
 def solution(mesh):
     n_pts, n_comp = mesh.shape["pts"], mesh.shape["comp"]
     n_chips = n_pts // CORES
@@ -513,9 +540,9 @@
                 V((sweeps, 1, n_loc), f32),
                 V((sweeps, 1, n_loc), f32),
                 V((4, kq, LANES), f32),
-                V((half, min(256, n_loc)), f32),
-                V((half, min(256, n_loc)), f32),
-                V((2, 4, kq, LANES), f32),
+                V((half, min(256, n_loc // 2)), f32),
+                V((half, min(256, n_loc // 2)), f32),
+                V((4, 4, kq, LANES), f32),
                 V((sweeps, 8, kq // 2, depth), f32),
                 V((sweeps, 6, kq // 2, depth), f32),
                 V((sweeps, 2, kq // 2, depth), f32),
@@ -525,13 +552,22 @@
                 V((4, 8, kq), f32),
                 pltpu.SemaphoreType.DMA((SINGLE + 8 + n_comp,)),
                 pltpu.SemaphoreType.DMA((ACROSS + sweeps * (n_comp - 1),)),
-                pltpu.SemaphoreType.DMA((7,)),
+                pltpu.SemaphoreType.DMA((10,)),
             ],
             compiler_params=pltpu.CompilerParams(
                 collective_id=0, has_side_effects=True, vmem_limit_bytes=44 * 1024 * 1024
             ),
             name="em",
         )(*(pltpu.with_memory_space_constraint(v, pltpu.HBM) for v in (inv_temp, points, means, log_w.reshape(n_pts, kq))))
+        copies = (mean, logw, lse)
+        mean, logw, lse = pl.pallas_call(
+            pass_kernel,
+            out_shape=tuple(pltpu.HBM(v.shape, f32) for v in copies),
+            in_specs=[vmem] * 3,
+            out_specs=(hbm,) * 3,
+            scratch_shapes=[pltpu.SemaphoreType.DMA((3,))],
+            name="results",
+        )(*(pltpu.with_memory_space_constraint(v, pltpu.VMEM) for v in copies))
         return mean, logw.reshape(k_loc), lse.reshape(n_loc)
 
     comp_spec = P(("fit", "comp"))

time: 91.1 us -> 91 us (level)
  local copies, waits for them, and re-layouts: 2.51 us -> 0 us
  Pallas kernels: 87.8 us -> 90.1 us
    unnamed x3 -> x0, local copies, waits for them, and re-layouts: 2.51 us -> none
    pallas_call x0 -> x1, Pallas kernels: none -> 1.35 us  [per_device(): pl.pallas_call(pass_kernel, out_shape=tuple((pltpu.HBM(v.shape, f32) for...]
where the time goes in v4:
time: 91 us; the launch traced here: 90.9 us
  Pallas kernels  90.1 us (99%)
    pallas_call x1, Pallas kernels, per_device(): pl.pallas_call(kernel, out_shape=(jax.ShapeDtypeStruct((k_loc, depth), f3...  88.7 us

profile of v4, /device:TPU:97, one launch (start us, length us, event | category | flops | bytes accessed | tf_op | source)
XLA Modules:
  0.0 90.9 jit_solution(12757143264501754433)
XLA Ops:
  0.6 88.7 %em.1 = (f32[1024,512]{1,0:T(8,128)S(1)}, f32[8,128]{1,0:T(8,128)S(1)}, f32[16,128]{1,0:T(8,128)S(1)}) custom-call(f32[3]{0:T(128)} %beta_hbm.1, bf16[2048,512]{1,0:T(8,128)(2,1)} %x_hbm.1, f32[1024,512]{1,0:T(8,128)} %mean_hbm.1, f32[8,128]{1,0:T(8,128)} %bitcast.3), custom_call_target="tpu_custom_call" | custom-call | tf_op jit(solution)/shard_map/em/pallas_call | solution.py:513
  89.3 1.4 %results.1 = (f32[1024,512]{1,0:T(8,128)}, f32[8,128]{1,0:T(8,128)}, f32[16,128]{1,0:T(8,128)}) custom-call(f32[1024,512]{1,0:T(8,128)S(1)} %get-tuple-element.9.mean_in, f32[8,128]{1,0:T(8,128)S(1)} %get-tuple-element.10.logw_in, f32[16,128]{1,0:T(8,128)S(1)} %get-tuple-element.11.lse_in), custom_call_target="tpu_custom_call" | custom-call | tf_op jit(solution)/shard_map/results/pallas_call | solution.py:563

commit v5 on v4

--- a/solution.py
+++ b/solution.py
@@ -16,7 +16,7 @@
 MESH = pl.DeviceIdType.MESH
 scope = contextlib.nullcontext
 CORES = 2
-PARTS = 4
+PARTS = 2
 DIRECT = 0
 LANES = 128
 
@@ -196,29 +196,25 @@
         s = sum(s_st[b:b + 1, cols] * jnp.exp2(ms[b] - m) for b in range(4))
         return m, s
 
-    chunk = n_loc // 2
-
-    def factors(h, lse):
-        cols = slice(h * n_loc, (h + 1) * n_loc)
-        factor[:, cols] = jnp.exp2(m_st[:, cols] - lse[...])
-
-    def r_phase(h, lo, c):
-        for b in (lo, lo + 1):
-            acc = jnp.zeros((kq, LANES), jnp.float32)
-            for at in range(h * n_loc + c * chunk, h * n_loc + (c + 1) * chunk, LANES):
-                cols = slice(at, at + LANES)
+    def r_phase(h, blocks, lse):
+        half_cols = slice(h * n_loc, (h + 1) * n_loc)
+        if 0 in blocks:
+            factor[:, half_cols] = jnp.exp2(m_st[:, half_cols] - lse[...])
+        accs = [jnp.zeros((kq, LANES), jnp.float32) for _ in blocks]
+        for c in range(n_loc // LANES):
+            cols = slice(h * n_loc + c * LANES, h * n_loc + (c + 1) * LANES)
+            for i, b in enumerate(blocks):
                 r = e_buf[b * kq:(b + 1) * kq, cols] * factor[b:b + 1, cols]
                 r_buf[b * kq:(b + 1) * kq, cols] = r.astype(jnp.bfloat16)
-                acc = acc + r
-            n_acc[2 * h + c, b] = acc
-
-    def stats(h, lo, c):
-        at = h * n_loc + c * chunk
+                accs[i] = accs[i] + r
+        for i, b in enumerate(blocks):
+            n_acc[h, b] = accs[i]
+
+    def stats(h, lo):
         out = jnp.dot(
-            r_buf[lo * kq:(lo + 2) * kq, at:at + chunk], x_all[h, c * chunk:(c + 1) * chunk],
-            preferred_element_type=jnp.float32,
+            r_buf[lo * kq:(lo + 2) * kq, h * n_loc:(h + 1) * n_loc], x_all[h], preferred_element_type=jnp.float32
         ).reshape(4, kh, depth)
-        if h == 0 and c == 0:
+        if h == 0:
             s_buf[t, 2 * lo:2 * lo + 4] = out
         else:
             s_buf[t, 2 * lo:2 * lo + 4] += out
@@ -286,20 +282,17 @@
             for i in range(n_loc // LANES):
                 lse_out[i:i + 1, :] = lse[:, i * LANES:(i + 1) * LANES]
 
-        with scope("rs_own"):
-            factors(0, lse_own.at[t])
-            r_phase(0, 0, 0)
-            r_phase(0, 0, 1)
-            stats(0, 0, 0)
+        own_r, oth_r = lse_own.at[t], lse_oth.at[t]
+        with scope("r_own_a"):
+            r_phase(0, (0, 1), own_r)
+        with scope("stats0"):
+            stats(0, 0)
         with scope("wait_swap"):
             swap.wait_recv()
+        with scope("r_oth_a"):
+            r_phase(1, (0, 1), oth_r)
         with scope("stats1"):
-            factors(1, lse_oth.at[t])
-            r_phase(1, 0, 0)
-            stats(0, 0, 1)
-            r_phase(1, 0, 1)
-            stats(1, 0, 0)
-            stats(1, 0, 1)
+            stats(1, 0)
 
         parts = [pl.ds(i * kp, kp) for i in range(PARTS)]
 
@@ -326,12 +319,11 @@
             wait_sums(t - 1)
         far_a, far_b, near_b = first_sends(core == 0)
         with scope("r_23"):
-            for h in range(2):
-                for c in range(2):
-                    r_phase(h, 2, c)
+            r_phase(0, (2, 3), own_r)
+            r_phase(1, (2, 3), oth_r)
         counts = []
         for b in range(4):
-            row = to_row(jnp.sum((n_acc[0, b] + n_acc[1, b]) + (n_acc[2, b] + n_acc[3, b]), axis=1, keepdims=True))
+            row = to_row(jnp.sum(n_acc[0, b] + n_acc[1, b], axis=1, keepdims=True))
             n_out[t, b, 0:1, :] = row
             counts.append(row)
         n_copies = [
@@ -339,9 +331,8 @@
             for d, (b, dev) in enumerate(((OPP, opposite), (RIGHT, right), (LEFT, left)))
         ]
         with scope("stats2"):
-            for h in range(2):
-                for c in range(2):
-                    stats(h, 2, c)
+            stats(0, 2)
+            stats(1, 2)
         first_sends(core == 1)
         near_a = [near_a_send(i) for i in range(2)]
         sum_a, sum_b = [], []
@@ -542,7 +533,7 @@
                 V((4, kq, LANES), f32),
                 V((half, min(256, n_loc // 2)), f32),
                 V((half, min(256, n_loc // 2)), f32),
-                V((4, 4, kq, LANES), f32),
+                V((2, 4, kq, LANES), f32),
                 V((sweeps, 8, kq // 2, depth), f32),
                 V((sweeps, 6, kq // 2, depth), f32),
                 V((sweeps, 2, kq // 2, depth), f32),

time: 91 us -> 90 us (0.989)
  Pallas kernels: 90.1 us -> 89.1 us
    pallas_call x1, Pallas kernels: 88.7 us -> 87.8 us  [per_device(): pl.pallas_call(kernel, out_shape=(jax.ShapeDtypeStruct((k_loc, depth), f3...]
where the time goes in v5:
time: 90 us; the launch traced here: 89.9 us
  Pallas kernels  89.1 us (99%)
    pallas_call x1, Pallas kernels, per_device(): pl.pallas_call(kernel, out_shape=(jax.ShapeDtypeStruct((k_loc, depth), f3...  87.8 us

profile of v5, /device:TPU:97, one launch (start us, length us, event | category | flops | bytes accessed | tf_op | source)
XLA Modules:
  0.0 89.9 jit_solution(6181006931365753576)
XLA Ops:
  0.6 87.8 %em.1 = (f32[1024,512]{1,0:T(8,128)S(1)}, f32[8,128]{1,0:T(8,128)S(1)}, f32[16,128]{1,0:T(8,128)S(1)}) custom-call(f32[3]{0:T(128)} %beta_hbm.1, bf16[2048,512]{1,0:T(8,128)(2,1)} %x_hbm.1, f32[1024,512]{1,0:T(8,128)} %mean_hbm.1, f32[8,128]{1,0:T(8,128)} %bitcast.3), custom_call_target="tpu_custom_call" | custom-call | tf_op jit(solution)/shard_map/em/pallas_call | solution.py:504
  88.4 1.4 %results.1 = (f32[1024,512]{1,0:T(8,128)}, f32[8,128]{1,0:T(8,128)}, f32[16,128]{1,0:T(8,128)}) custom-call(f32[1024,512]{1,0:T(8,128)S(1)} %get-tuple-element.9.mean_in, f32[8,128]{1,0:T(8,128)S(1)} %get-tuple-element.10.logw_in, f32[16,128]{1,0:T(8,128)S(1)} %get-tuple-element.11.lse_in), custom_call_target="tpu_custom_call" | custom-call | tf_op jit(solution)/shard_map/results/pallas_call | solution.py:554

commit v6 on v5

--- a/solution.py
+++ b/solution.py
@@ -22,6 +22,8 @@
 
 OPP, RIGHT, LEFT, OWN = range(4)
 SHIFT = {OPP: 2, RIGHT: 1, LEFT: 3, OWN: 0}
+ORDER = [(OPP, 0), (OPP, 1), (RIGHT, 1), (LEFT, 0), (RIGHT, 0), (LEFT, 1), (OWN, 0), (OWN, 1)]
+PLACE = {piece: i for i, piece in enumerate(ORDER)}
 
 PAIR, SWAP, COUNT, ROW, FINAL, XPART, PIECES = 0, 1, 2, 5, 9, 10, 14
 FAR_A, FAR_B, NEAR_A, NEAR_B, SUM_A, SUM_B, OWN_A_RIGHT, OWN_B_RIGHT, OWN_A_LEFT, OWN_B_LEFT, ON_A, ON_B = range(
@@ -62,7 +64,7 @@
     for dev in everyone:
         pl.semaphore_signal(barrier, inc=1, device_id=dev, device_id_type=MESH)
 
-    tr = min(512, n_loc // 2)
+    tr = min(1024, n_loc // 2)
     n_tr = n_loc // tr
     x_rows = [pl.ds(c * tr, tr) for c in range(n_tr)]
     load_x = [pltpu.make_async_copy(x_hbm.at[r], x_all.at[0, r], copy_sem.at[6 + c]) for c, r in enumerate(x_rows)]
@@ -139,7 +141,7 @@
             prm[0, b, 0:1, :] = logw_ref[pl.ds(core * n_chips + q, 1), :]
             prm[0, b, 1:2, :] = to_row(jnp.sum(mf * mf, axis=1, keepdims=True))
 
-    tile = min(256, n_loc // 2)
+    tile = min(512, n_loc // 2)
 
     def prepare(u):
         h, at = divmod(u * tile, n_loc)
@@ -182,7 +184,9 @@
                     logit = a * slope + cols_c[b]
                     m = jnp.max(logit, axis=0, keepdims=True)
                     e = jnp.exp2(logit - m)
-                    e_buf[b * kq:(b + 1) * kq, cols] = e
+                    for half_b in range(2):
+                        at_row = PLACE[b, half_b] * kh
+                        e_buf[at_row:at_row + kh, cols] = e[half_b * kh:(half_b + 1) * kh]
                     m_st[b:b + 1, cols] = m
                     s_st[b:b + 1, cols] = jnp.sum(e, axis=0, keepdims=True)
 
@@ -196,28 +200,31 @@
         s = sum(s_st[b:b + 1, cols] * jnp.exp2(ms[b] - m) for b in range(4))
         return m, s
 
-    def r_phase(h, blocks, lse):
+    def r_phase(h, group, lse):
         half_cols = slice(h * n_loc, (h + 1) * n_loc)
-        if 0 in blocks:
+        if group == 0:
             factor[:, half_cols] = jnp.exp2(m_st[:, half_cols] - lse[...])
-        accs = [jnp.zeros((kq, LANES), jnp.float32) for _ in blocks]
+        places = range(4 * group, 4 * group + 4)
+        accs = [jnp.zeros((kh, LANES), jnp.float32) for _ in places]
         for c in range(n_loc // LANES):
             cols = slice(h * n_loc + c * LANES, h * n_loc + (c + 1) * LANES)
-            for i, b in enumerate(blocks):
-                r = e_buf[b * kq:(b + 1) * kq, cols] * factor[b:b + 1, cols]
-                r_buf[b * kq:(b + 1) * kq, cols] = r.astype(jnp.bfloat16)
+            for i, place in enumerate(places):
+                b = ORDER[place][0]
+                r = e_buf[place * kh:(place + 1) * kh, cols] * factor[b:b + 1, cols]
+                r_buf[place * kh:(place + 1) * kh, cols] = r.astype(jnp.bfloat16)
                 accs[i] = accs[i] + r
-        for i, b in enumerate(blocks):
-            n_acc[h, b] = accs[i]
-
-    def stats(h, lo):
+        for i, place in enumerate(places):
+            n_acc[h, place] = accs[i]
+
+    def stats(h, group):
+        rows = slice(4 * group * kh, 4 * (group + 1) * kh)
         out = jnp.dot(
-            r_buf[lo * kq:(lo + 2) * kq, h * n_loc:(h + 1) * n_loc], x_all[h], preferred_element_type=jnp.float32
+            r_buf[rows, h * n_loc:(h + 1) * n_loc], x_all[h], preferred_element_type=jnp.float32
         ).reshape(4, kh, depth)
         if h == 0:
-            s_buf[t, 2 * lo:2 * lo + 4] = out
+            s_buf[t, 4 * group:4 * group + 4] = out
         else:
-            s_buf[t, 2 * lo:2 * lo + 4] += out
+            s_buf[t, 4 * group:4 * group + 4] += out
 
     for t in range(sweeps):
         last = t == sweeps - 1
@@ -284,20 +291,20 @@
 
         own_r, oth_r = lse_own.at[t], lse_oth.at[t]
         with scope("r_own_a"):
-            r_phase(0, (0, 1), own_r)
+            r_phase(0, 0, own_r)
         with scope("stats0"):
             stats(0, 0)
         with scope("wait_swap"):
             swap.wait_recv()
         with scope("r_oth_a"):
-            r_phase(1, (0, 1), oth_r)
+            r_phase(1, 0, oth_r)
         with scope("stats1"):
             stats(1, 0)
 
         parts = [pl.ds(i * kp, kp) for i in range(PARTS)]
 
         def s_piece(b, half_b, i):
-            return s_buf.at[t, 2 * b + half_b, parts[i]]
+            return s_buf.at[t, PLACE[b, half_b], parts[i]]
 
         def in_piece(slot, i):
             return rs_in.at[t, slot, parts[i]]
@@ -305,25 +312,26 @@
         def near_b_send(i, when=None):
             return send(s_piece(RIGHT, 1, i), in_piece(2, i), NEAR_B + i, SUMS_RIGHT, right, when)
 
-        def near_a_send(i):
-            return send(s_piece(LEFT, 0, i), in_piece(3, i), NEAR_A + i, SUMS_LEFT, left)
+        def near_a_send(i, when=None):
+            return send(s_piece(LEFT, 0, i), in_piece(3, i), NEAR_A + i, SUMS_LEFT, left, when)
 
         def first_sends(when):
             a, b = [], []
             for i in range(PARTS):
                 a.append(send(s_piece(OPP, 0, i), in_piece(0, i), FAR_A + i, SUMS_RIGHT, right, when))
                 b.append(send(s_piece(OPP, 1, i), in_piece(1, i), FAR_B + i, SUMS_LEFT, left, when))
-            return a, b, [near_b_send(i, when) for i in range(2)]
+            return a, b, [near_b_send(i, when) for i in range(2)], [near_a_send(i, when) for i in range(2)]
 
         if t > 0:
             wait_sums(t - 1)
-        far_a, far_b, near_b = first_sends(core == 0)
+        far_a, far_b, near_b, near_a = first_sends(core == 0)
         with scope("r_23"):
-            r_phase(0, (2, 3), own_r)
-            r_phase(1, (2, 3), oth_r)
+            r_phase(0, 1, own_r)
+            r_phase(1, 1, oth_r)
         counts = []
         for b in range(4):
-            row = to_row(jnp.sum(n_acc[0, b] + n_acc[1, b], axis=1, keepdims=True))
+            by_lane = [n_acc[0, PLACE[b, half_b]] + n_acc[1, PLACE[b, half_b]] for half_b in range(2)]
+            row = to_row(jnp.sum(jnp.concatenate(by_lane, axis=0), axis=1, keepdims=True))
             n_out[t, b, 0:1, :] = row
             counts.append(row)
         n_copies = [
@@ -331,21 +339,20 @@
             for d, (b, dev) in enumerate(((OPP, opposite), (RIGHT, right), (LEFT, left)))
         ]
         with scope("stats2"):
-            stats(0, 2)
-            stats(1, 2)
+            stats(0, 1)
+            stats(1, 1)
         first_sends(core == 1)
-        near_a = [near_a_send(i) for i in range(2)]
         sum_a, sum_b = [], []
         for i in range(PARTS):
             with scope("wait_far_a"):
                 far_a[i].wait_recv()
-            acc_out[t, 0, parts[i]] = s_buf[t, 2 * RIGHT, parts[i]] + rs_in[t, 0, parts[i]]
+            acc_out[t, 0, parts[i]] = s_buf[t, PLACE[RIGHT, 0], parts[i]] + rs_in[t, 0, parts[i]]
             sum_a.append(send(acc_out.at[t, 0, parts[i]], in_piece(4, i), SUM_A + i, SUMS_RIGHT, right))
             if i + 2 < PARTS:
                 near_b.append(near_b_send(i + 2))
             with scope("wait_far_b"):
                 far_b[i].wait_recv()
-            acc_out[t, 1, parts[i]] = s_buf[t, 2 * LEFT + 1, parts[i]] + rs_in[t, 1, parts[i]]
+            acc_out[t, 1, parts[i]] = s_buf[t, PLACE[LEFT, 1], parts[i]] + rs_in[t, 1, parts[i]]
             sum_b.append(send(acc_out.at[t, 1, parts[i]], in_piece(5, i), SUM_B + i, SUMS_LEFT, left))
             if i + 2 < PARTS:
                 near_a.append(near_a_send(i + 2))
@@ -396,7 +403,7 @@
                     far[i].wait_recv()
                 at = half_b * kh + i * kp
                 mean = (
-                    s_buf[t, 2 * OWN + half_b, parts[i]] + rs_in[t, slots[0], parts[i]] + rs_in[t, slots[1], parts[i]]
+                    s_buf[t, PLACE[OWN, half_b], parts[i]] + rs_in[t, slots[0], parts[i]] + rs_in[t, slots[1], parts[i]]
                 ) / n_col[at:at + kp]
                 m_piece(OWN, half_b, i)[...] = mean if last else mean.astype(jnp.bfloat16)
                 sq[half_b, i] = jnp.sum(mean * mean, axis=1, keepdims=True)
@@ -531,9 +538,9 @@
                 V((sweeps, 1, n_loc), f32),
                 V((sweeps, 1, n_loc), f32),
                 V((4, kq, LANES), f32),
-                V((half, min(256, n_loc // 2)), f32),
-                V((half, min(256, n_loc // 2)), f32),
-                V((2, 4, kq, LANES), f32),
+                V((half, min(512, n_loc // 2)), f32),
+                V((half, min(512, n_loc // 2)), f32),
+                V((2, 8, kq // 2, LANES), f32),
                 V((sweeps, 8, kq // 2, depth), f32),
                 V((sweeps, 6, kq // 2, depth), f32),
                 V((sweeps, 2, kq // 2, depth), f32),

time: 90 us -> 90 us (level)
  no operation moved by 1% of the time
where the time goes in v6:
time: 90 us; the launch traced here: 89.9 us
  Pallas kernels  89.1 us (99%)
    pallas_call x1, Pallas kernels, per_device(): pl.pallas_call(kernel, out_shape=(jax.ShapeDtypeStruct((k_loc, depth), f3...  87.8 us

profile of v6, /device:TPU:97, one launch (start us, length us, event | category | flops | bytes accessed | tf_op | source)
XLA Modules:
  0.0 89.9 jit_solution(5933336190161140861)
XLA Ops:
  0.6 87.8 %em.1 = (f32[1024,512]{1,0:T(8,128)S(1)}, f32[8,128]{1,0:T(8,128)S(1)}, f32[16,128]{1,0:T(8,128)S(1)}) custom-call(f32[3]{0:T(128)} %beta_hbm.1, bf16[2048,512]{1,0:T(8,128)(2,1)} %x_hbm.1, f32[1024,512]{1,0:T(8,128)} %mean_hbm.1, f32[8,128]{1,0:T(8,128)} %bitcast.3), custom_call_target="tpu_custom_call" | custom-call | tf_op jit(solution)/shard_map/em/pallas_call | solution.py:511
  88.4 1.4 %results.1 = (f32[1024,512]{1,0:T(8,128)}, f32[8,128]{1,0:T(8,128)}, f32[16,128]{1,0:T(8,128)}) custom-call(f32[1024,512]{1,0:T(8,128)S(1)} %get-tuple-element.9.mean_in, f32[8,128]{1,0:T(8,128)S(1)} %get-tuple-element.10.logw_in, f32[16,128]{1,0:T(8,128)S(1)} %get-tuple-element.11.lse_in), custom_call_target="tpu_custom_call" | custom-call | tf_op jit(solution)/shard_map/results/pallas_call | solution.py:561
